TPU v7x, 128 devices: a whole 4x4x4 slice. The times are simulated.
128 devices in a mesh: tp: 16 (over z, y), dp: 8 (over x, core).
Axes of the slice: x: 4, y: 4, z: 4, core: 2. Of those that a mesh axis runs over, the one named last changes fastest.
Arguments:
- x_in: bfloat16 [2048, 4096], P(('dp', 'tp'))
- w_gate: bfloat16 [4096, 16384], P('dp', 'tp')
- w_up: bfloat16 [4096, 16384], P('dp', 'tp')
- w_down: bfloat16 [16384, 4096], P('tp', 'dp')
- grad_y: bfloat16 [2048, 4096], P(('dp', 'tp'))
Outputs:
- output 1: bfloat16 [2048, 4096], P(('dp', 'tp'))
- output 2: bfloat16 [2048, 4096], P(('dp', 'tp'))
- output 3: float32 [4096, 16384], P('dp', 'tp')
- output 4: float32 [4096, 16384], P('dp', 'tp')
- output 5: float32 [16384, 4096], P('tp', 'dp')
All inputs are finite; a program needn't handle non-finite values.
Results may differ from a plain program's by a relative error of at most 0.00141.
Values are sent between devices in bfloat16 or wider.
A program may use at most 1 GiB of HBM per device.

v0:
```python
import jax
import jax.numpy as jnp
from jax import lax
from jax.sharding import PartitionSpec as P


def solution(mesh):
    dp_size = mesh.shape["dp"]
    tp_size = mesh.shape["tp"]

    def spread_cols(rows_loc):
        tok_dev = rows_loc.shape[0]
        cols_mine = lax.all_to_all(rows_loc, "dp", 1, 0, tiled=True)
        col_width = cols_mine.shape[1]
        cols_mine = cols_mine.reshape(dp_size, tok_dev, col_width)
        gathered = lax.all_gather(cols_mine, "tp", axis=1)
        return cols_mine, gathered.reshape(dp_size * tp_size * tok_dev, col_width)

    def collect_rows(col_part, resid):
        tok_dev = resid.shape[1]
        col_width = col_part.shape[1]
        summed = lax.psum_scatter(col_part.reshape(dp_size, tp_size, tok_dev, col_width), "tp", scatter_dimension=1, tiled=True)
        summed = summed.reshape(dp_size, tok_dev, col_width) + resid.astype(jnp.float32)
        out_rows = lax.all_to_all(summed.astype(jnp.bfloat16), "dp", 0, 2, tiled=True)
        return out_rows.reshape(tok_dev, dp_size * col_width)

    def local_step(x_loc, wg_loc, wu_loc, wd_loc, gy_loc):
        x_mine, x_cols = spread_cols(x_loc)
        gate_pre = lax.psum_scatter(jnp.dot(x_cols, wg_loc, preferred_element_type=jnp.float32), "dp", scatter_dimension=0, tiled=True)
        up_pre = lax.psum_scatter(jnp.dot(x_cols, wu_loc, preferred_element_type=jnp.float32), "dp", scatter_dimension=0, tiled=True)
        sig_gate = jax.nn.sigmoid(gate_pre)
        silu_gate = gate_pre * sig_gate
        hidden = (silu_gate * up_pre).astype(jnp.bfloat16)
        hidden_all = lax.all_gather(hidden, "dp", axis=0, tiled=True)
        y_rows = collect_rows(jnp.dot(hidden_all, wd_loc, preferred_element_type=jnp.float32), x_mine)

        gy_mine, gy_cols = spread_cols(gy_loc)
        grad_h = lax.psum_scatter(jnp.einsum("nd,fd->nf", gy_cols, wd_loc, preferred_element_type=jnp.float32), "dp", scatter_dimension=0, tiled=True)
        grad_wd = jnp.einsum("nf,nd->fd", hidden_all, gy_cols, preferred_element_type=jnp.float32)
        silu_deriv = sig_gate * (1.0 + gate_pre * (1.0 - sig_gate))
        grad_gate = (grad_h * up_pre * silu_deriv).astype(jnp.bfloat16)
        grad_up = (grad_h * silu_gate).astype(jnp.bfloat16)
        gate_all = lax.all_gather(grad_gate, "dp", axis=0, tiled=True)
        up_all = lax.all_gather(grad_up, "dp", axis=0, tiled=True)
        grad_wg = jnp.einsum("nd,nf->df", x_cols, gate_all, preferred_element_type=jnp.float32)
        grad_wu = jnp.einsum("nd,nf->df", x_cols, up_all, preferred_element_type=jnp.float32)
        gx_part = (jnp.einsum("nf,df->nd", gate_all, wg_loc, preferred_element_type=jnp.float32)
                   + jnp.einsum("nf,df->nd", up_all, wu_loc, preferred_element_type=jnp.float32))
        gx_rows = collect_rows(gx_part, gy_mine)
        return y_rows, gx_rows, grad_wg, grad_wu, grad_wd

    row_spec = P(("dp", "tp"), None)
    up_spec = P("dp", "tp")
    down_spec = P("tp", "dp")
    return jax.shard_map(local_step, mesh=mesh,
                         in_specs=(row_spec, up_spec, up_spec, down_spec, row_spec),
                         out_specs=(row_spec, row_spec, up_spec, up_spec, down_spec),
                         check_vma=False)
```

profile of v0, /device:TPU:1, one launch (start us, length us, event | category | flops | bytes accessed | tf_op | source)
XLA Modules:
  0.0 564.0 jit_solution(14988832531881198177)
XLA Ops:
  7.2 1.0 copy.50
  8.2 10.8 %all_to_all.62 = bf16[16,8,512]{2,0,1:T(8,128)(2,1)S(1)} all-to-all(bf16[16,8,512]{2,0,1:T(8,128)(2,1)S(1)} %bitcast.83), channel_id=1, replica_groups=mesh['tp'=16,'dp'=8] {'dp'}, dimensions={1} | all-to-all | bytes 262144 | tf_op jit(solution)/shard_map/all_to_all | solution.py:13
  19.9 0.9 copy.51
  20.8 8.5 %all_to_all.63 = bf16[16,8,512]{2,0,1:T(8,128)(2,1)S(1)} all-to-all(bf16[16,8,512]{2,0,1:T(8,128)(2,1)S(1)} %bitcast.84), channel_id=1, replica_groups=mesh['tp'=16,'dp'=8] {'dp'}, dimensions={1} | all-to-all | bytes 262144 | tf_op jit(solution)/shard_map/all_to_all | solution.py:13
  30.1 33.9 %all-gather.16.cloned.1.call-done = bf16[8,256,512]{2,0,1:T(8,128)(2,1)} async-done(((bf16[8,16,512]{2,0,1:T(8,128)(2,1)}), bf16[8,256,512]{2,0,1:T(8,128)(2,1)}) %all-gather.16.cloned.1.call-update) | async-done | bytes 2097168 | tf_op jit(solution)/shard_map/all_gather | solution.py:16
  63.9 2.3 copy.34
  66.2 5.7 %fusion.8 = f32[2048,1024]{1,0:T(8,128)} fusion(bf16[2048,512]{1,0:T(8,128)(2,1)S(1)} %bitcast.75, bf16[1024,512]{1,0:T(8,128)(2,1)S(1)} %copy-done), kind=kOutput, calls=%fused_computation.19 | convolution fusion | flops 2147483648 | bytes 11534336 | tf_op jit(solution)/shard_map/nd,fd->nf/dot_general | solution.py:38
  72.0 39.0 %all-gather.14.cloned.1.call-done = bf16[8,256,512]{2,0,1:T(8,128)(2,1)} async-done(((bf16[8,16,512]{2,0,1:T(8,128)(2,1)}), bf16[8,256,512]{2,0,1:T(8,128)(2,1)}) %all-gather.14.cloned.1.call-update) | async-done | bytes 2097168 | tf_op jit(solution)/shard_map/all_gather | solution.py:16
  111.0 2.3 copy.30
  113.4 5.6 fusion.6
  119.0 6.8 %fusion.5 = f32[2048,1024]{1,0:T(8,128)} fusion(bf16[2048,512]{1,0:T(8,128)(2,1)S(1)} %bitcast.72, bf16[512,1024]{1,0:T(8,128)(2,1)} %param.6), kind=kOutput, calls=%fused_computation.16 | convolution fusion | flops 2147483648 | bytes 11534336 | tf_op jit(solution)/shard_map/dot_general | solution.py:29
  125.9 40.6 %reduce-scatter.10.cloned.1.call-done = f32[256,1024]{1,0:T(8,128)} async-done(((f32[2048,1024]{1,0:T(8,128)}), f32[256,1024]{1,0:T(8,128)}) %reduce-scatter.10.cloned.1.call-update) | async-done | bytes 1048592 | tf_op jit(solution)/shard_map/reduce_scatter | solution.py:38
  166.5 54.5 %reduce-scatter.8.cloned.1.call-done = f32[256,1024]{1,0:T(8,128)} async-done(((f32[2048,1024]{1,0:T(8,128)}), f32[256,1024]{1,0:T(8,128)}) %reduce-scatter.8.cloned.1.call-update) | async-done | bytes 1048592 | tf_op jit(solution)/shard_map/reduce_scatter | solution.py:30
  221.0 54.5 %reduce-scatter.6.cloned.1.call-done = f32[256,1024]{1,0:T(8,128)} async-done(((f32[2048,1024]{1,0:T(8,128)}), f32[256,1024]{1,0:T(8,128)}) %reduce-scatter.6.cloned.1.call-update) | async-done | bytes 1048592 | tf_op jit(solution)/shard_map/reduce_scatter | solution.py:29
  275.4 3.8 multiply_convert_fusion
  281.0 30.8 %all-gather.8.cloned.1.call-done = bf16[2048,1024]{1,0:T(8,128)(2,1)} async-done(((bf16[256,1024]{1,0:T(8,128)(2,1)}), bf16[2048,1024]{1,0:T(8,128)(2,1)}) %all-gather.8.cloned.1.call-update) | async-done | bytes 4194320 | tf_op jit(solution)/shard_map/all_gather | solution.py:34
  311.8 6.5 %fusion.7 = f32[2048,512]{1,0:T(8,128)} fusion(bf16[2048,1024]{1,0:T(8,128)(2,1)} %all-gather.8.cloned.1.call-done, bf16[1024,512]{1,0:T(8,128)(2,1)S(1)} %copy-done), kind=kOutput, calls=%fused_computation.18 | convolution fusion | flops 2147483648 | bytes 9437184 | tf_op jit(solution)/shard_map/dot_general | solution.py:35
  318.3 27.6 %all-gather.10.cloned.1.call-done = bf16[2048,1024]{1,0:T(8,128)(2,1)} async-done(((bf16[256,1024]{1,0:T(8,128)(2,1)}), bf16[2048,1024]{1,0:T(8,128)(2,1)}) %all-gather.10.cloned.1.call-update) | async-done | bytes 4194320 | tf_op jit(solution)/shard_map/all_gather | solution.py:43
  345.8 6.9 %fusion.9 = f32[2048,512]{1,0:T(8,128)} fusion(bf16[2048,1024]{1,0:T(8,128)(2,1)} %all-gather.10.cloned.1.call-done, bf16[512,1024]{1,0:T(8,128)(2,1)} %param.6), kind=kOutput, calls=%fused_computation.20 | convolution fusion | flops 2147483648 | bytes 9437184 | tf_op jit(solution)/shard_map/nf,df->nd/dot_general | solution.py:47
  352.7 27.2 %all-gather.12.cloned.1.call-done = bf16[2048,1024]{1,0:T(8,128)(2,1)} async-done(((bf16[256,1024]{1,0:T(8,128)(2,1)}), bf16[2048,1024]{1,0:T(8,128)(2,1)}) %all-gather.12.cloned.1.call-update) | async-done | bytes 4194320 | tf_op jit(solution)/shard_map/all_gather | solution.py:44
  379.9 7.8 %convolution_add_fusion = f32[2048,512]{1,0:T(8,128)} fusion(f32[2048,512]{1,0:T(8,128)} %fusion.9, bf16[2048,1024]{1,0:T(8,128)(2,1)} %all-gather.12.cloned.1.call-done, bf16[512,1024]{1,0:T(8,128)(2,1)S(1)} %copy-done.6), kind=kOutput, calls=%fused_computation | convolution fusion | flops 2148532224 | bytes 13631488 | tf_op jit(solution)/shard_map/nf,df->nd/dot_general | solution.py:48
  389.0 6.7 %fusion.10 = f32[1024,512]{1,0:T(8,128)} fusion(bf16[2048,1024]{1,0:T(8,128)(2,1)} %all-gather.8.cloned.1.call-done, bf16[2048,512]{1,0:T(8,128)(2,1)} %bitcast.76), kind=kOutput, calls=%fused_computation.21 | convolution fusion | flops 2147483648 | bytes 8388608 | tf_op jit(solution)/shard_map/nf,nd->fd/dot_general | solution.py:39
  395.7 3.7 convolution_bitcast_fusion.1
  399.4 128.8 %all-reduce.5.cloned.1.call-done = (f32[8,16,16,512]{3,2,1,0:T(8,128)}, f32[8,16,16,512]{3,2,1,0:T(8,128)}) async-done(((f32[8,16,16,512]{3,2,1,0:T(8,128)}, f32[8,16,16,512]{3,2,1,0:T(8,128)}), (f32[8,16,16,512]{3,2,1,0:T(8,128)}, f32[8,16,16,512]{3,2,1,0:T(8,128)})) %all-reduce.5.cloned.1.call-update) | async-done | bytes 8388624
  528.1 2.3 fusion.2
  530.4 5.7 %all-to-all-start.3 = ((bf16[8,16,512]{2,1,0:T(8,128)(2,1)}), bf16[8,16,512]{2,1,0:T(8,128)(2,1)S(1)}, u32[]{:S(2)}, u32[]{:S(2)}) async-start(bf16[8,16,512]{2,1,0:T(8,128)(2,1)} %fusion.2), calls=%async_computation.6 | async-start | bytes 262144 | tf_op jit(solution)/shard_map/all_to_all | solution.py:24
  536.1 2.3 fusion.4
  538.4 2.8 all-to-all-done.3
  541.1 4.1 all-to-all-start.1
  545.3 6.0 %convolution_bitcast_fusion = f32[512,1024]{0,1:T(8,128)} fusion(bf16[2048,1024]{1,0:T(8,128)(2,1)} %all-gather.12.cloned.1.call-done, bf16[2048,512]{1,0:T(8,128)(2,1)S(1)} %bitcast.74), kind=kOutput, calls=%fused_computation.1 | convolution fusion | flops 2147483648 | bytes 8388608 | tf_op jit(solution)/shard_map/nd,nf->df/dot_general | solution.py:46
  551.3 3.0 copy.37
  554.3 1.8 copy.36
  (40 shorter events, 6.1 us)
Async XLA Ops:
  7.2 59.1 %copy-start = (bf16[1024,512]{1,0:T(8,128)(2,1)S(1)}, bf16[1024,512]{1,0:T(8,128)(2,1)}, u32[]{:S(2)}) copy-start(bf16[1024,512]{1,0:T(8,128)(2,1)} %param.8) | copy-start | bytes 3145732
  7.2 56.8 %all-gather.16.cloned.1.call-start = ((), (), s32[]{:S(2)}) async-start(), calls=%async_computation.14 | async-start | bytes 2228224 | tf_op jit(solution)/shard_map/all_gather | solution.py:16
  19.8 91.2 %all-gather.14.cloned.1.call-start = ((), (), s32[]{:S(2)}) async-start(), calls=%async_computation.13 | async-start | bytes 2228224 | tf_op jit(solution)/shard_map/all_gather | solution.py:16
  30.0 136.5 %reduce-scatter.10.cloned.1.call-start = ((), (), s32[]{:S(2)}) async-start(), calls=%async_computation.10 | async-start | bytes 9437184 | tf_op jit(solution)/shard_map/reduce_scatter | solution.py:38
  66.2 5.8 %copy-start.2 = (bf16[8,256,512]{2,1,0:T(8,128)(2,1)}, bf16[8,256,512]{2,1,0:T(8,128)(2,1)S(1)}, u32[]{:S(2)}) copy-start(bf16[8,256,512]{2,1,0:T(8,128)(2,1)S(1)} %copy.34) | copy-start | bytes 6291460
  71.9 149.1 %reduce-scatter.8.cloned.1.call-start = ((), (), s32[]{:S(2)}) async-start(), calls=%async_computation.8 | async-start | bytes 9437184 | tf_op jit(solution)/shard_map/reduce_scatter | solution.py:30
  111.0 2.4 copy-start.5
  118.9 156.5 %reduce-scatter.6.cloned.1.call-start = ((), (), s32[]{:S(2)}) async-start(), calls=%async_computation.7 | async-start | bytes 9437184 | tf_op jit(solution)/shard_map/reduce_scatter | solution.py:29
  125.9 185.9 %all-gather.8.cloned.1.call-start = ((), (), s32[]{:S(2)}) async-start(), calls=%async_computation.9 | async-start | bytes 4718592 | tf_op jit(solution)/shard_map/all_gather | solution.py:34
  279.3 66.5 %all-gather.10.cloned.1.call-start = ((), (), s32[]{:S(2)}) async-start(), calls=%async_computation.11 | async-start | bytes 4718592 | tf_op jit(solution)/shard_map/all_gather | solution.py:43
  280.0 99.8 %all-gather.12.cloned.1.call-start = ((), (), s32[]{:S(2)}) async-start(), calls=%async_computation.12 | async-start | bytes 4718592 | tf_op jit(solution)/shard_map/all_gather | solution.py:44
  280.8 247.3 %all-reduce.5.cloned.1.call-start = ((), (), s32[]{:S(2)}) async-start(), calls=%async_computation.15 | async-start | bytes 16777216
  318.3 61.6 %copy-start.6 = (bf16[512,1024]{1,0:T(8,128)(2,1)S(1)}, bf16[512,1024]{1,0:T(8,128)(2,1)}, u32[]{:S(2)}) copy-start(bf16[512,1024]{1,0:T(8,128)(2,1)} %param.7) | copy-start | bytes 3145732
  387.7 0.7 copy-start.7
  389.0 6.7 %copy-start.4 = (bf16[2048,1024]{1,0:T(8,128)(2,1)S(1)}, bf16[2048,1024]{1,0:T(8,128)(2,1)}, u32[]{:S(2)}) copy-start(bf16[2048,1024]{1,0:T(8,128)(2,1)} %all-gather.10.cloned.1.call-done) | copy-start | bytes 12582916
  530.4 10.8 %all-to-all-start.3 = ((bf16[8,16,512]{2,1,0:T(8,128)(2,1)}), bf16[8,16,512]{2,1,0:T(8,128)(2,1)S(1)}, u32[]{:S(2)}, u32[]{:S(2)}) async-start(bf16[8,16,512]{2,1,0:T(8,128)(2,1)} %fusion.2), calls=%async_computation.6 | async-start | bytes 262144 | tf_op jit(solution)/shard_map/all_to_all | solution.py:24
  541.1 15.6 %all-to-all-start.1 = ((bf16[8,16,512]{2,1,0:T(8,128)(2,1)}), bf16[8,16,512]{2,1,0:T(8,128)(2,1)S(1)}, u32[]{:S(2)}, u32[]{:S(2)}) async-start(bf16[8,16,512]{2,1,0:T(8,128)(2,1)} %fusion.4), calls=%async_computation.3 | async-start | bytes 262144 | tf_op jit(solution)/shard_map/all_to_all | solution.py:24
  545.3 12.2 %copy-start.1 = (bf16[1024,512]{1,0:T(8,128)(2,1)S(1)}, bf16[1024,512]{1,0:T(8,128)(2,1)}, u32[]{:S(2)}) copy-start(bf16[1024,512]{1,0:T(8,128)(2,1)} %param.8) | copy-start | bytes 3145732
  551.3 3.0 copy-start.3
Sparse Core Ops, SparseCore 0:
  19.9 43.9 all-gather.15
  66.7 44.2 all-gather.13
  113.4 53.0 reduce-scatter.9
  168.8 52.1 reduce-scatter.7
  223.2 52.1 reduce-scatter.5
  279.4 32.3 all-gather.7
  314.1 31.7 all-gather.9
  348.1 31.7 all-gather.11
  387.9 140.1 all-reduce.4
where the time goes:
time: 565 us; the launch traced here: 564 us
  waiting for transfers between devices  441 us (78%)
  matrix products  55.6 us (10%)
  blocking collectives  19.3 us (3%)
  local copies, waits for them, and re-layouts  15.4 us (3%)
  between operations  13.9 us (2%)
  starting transfers between devices  10.4 us (2%)
  other arithmetic  8.36 us (1%)
    unnamed x10, waiting for transfers between devices  130 us
    all_gather x2, waiting for transfers between devices, spread_cols(): gathered = lax.all_gather(cols_mine, 'tp', axis=1)  72.9 us
    reduce_scatter x1, waiting for transfers between devices, local_step(): lax.psum_scatter(jnp.dot(x_cols, wu_loc, preferred_element_type=jnp.float...  54.5 us
    reduce_scatter x1, waiting for transfers between devices, local_step(): lax.psum_scatter(jnp.dot(x_cols, wg_loc, preferred_element_type=jnp.float...  54.5 us
    reduce_scatter x1, waiting for transfers between devices, local_step(): lax.psum_scatter(jnp.einsum('nd,fd->nf', gy_cols, wd_loc, preferred_eleme...  40.6 us
    all_gather x1, waiting for transfers between devices, local_step(): hidden_all = lax.all_gather(hidden, 'dp', axis=0, tiled=True)  30.8 us
    all_gather x1, waiting for transfers between devices, local_step(): gate_all = lax.all_gather(grad_gate, 'dp', axis=0, tiled=True)  27.6 us
    all_gather x1, waiting for transfers between devices, local_step(): up_all = lax.all_gather(grad_up, 'dp', axis=0, tiled=True)  27.2 us
  transfers between devices with their start and end apart: 11, of which 10 were waited for; matrix products, arithmetic and copies ran while one was open for 11% of the time, Pallas kernels for 0%

commit v1 on v0

v1 whole, which is shorter than its diff:
```python
import jax
import jax.numpy as jnp
from jax import lax
from jax.experimental import pallas as pl
from jax.experimental.pallas import tpu as pltpu
from jax.sharding import PartitionSpec as P

RING = 4
N_DP = 2 * RING
VMEM = pltpu.MemorySpace.VMEM


class Links:
    def __init__(self, send_sem, recv_sem, local_sem):
        self.send_sem, self.recv_sem, self.local_sem = send_sem, recv_sem, local_sem
        self.n_remote = self.n_local = 0
        self.sent, self.local = [], []
        dp, tp = lax.axis_index("dp"), lax.axis_index("tp")
        self.dp, self.tp = dp, tp
        self.x, self.core = dp // 2, dp % 2
        self.z, self.y = tp // RING, tp % RING

    def at(self, pos, off):
        return (pos + off) % RING

    def device(self, axis, off):
        if axis == "x":
            return {"dp": 2 * self.at(self.x, off) + self.core, "tp": self.tp}
        if axis == "core":
            return {"dp": 2 * self.x + (1 - self.core), "tp": self.tp}
        if axis == "dp":
            return {"dp": (self.dp + off) % N_DP, "tp": self.tp}
        if axis == "z":
            return {"dp": self.dp, "tp": RING * self.at(self.z, off) + self.y}
        return {"dp": self.dp, "tp": RING * self.z + self.at(self.y, off)}

    def barrier(self, peers):
        sem = pltpu.get_barrier_semaphore()
        for axis, off in peers:
            pl.semaphore_signal(sem, inc=1, device_id=self.device(axis, off),
                                device_id_type=pl.DeviceIdType.MESH)
        pl.semaphore_wait(sem, len(peers))

    def send(self, src, dst, axis, off=0):
        k = self.n_remote
        self.n_remote += 1
        copy = pltpu.make_async_remote_copy(
            src_ref=src, dst_ref=dst, send_sem=self.send_sem.at[k], recv_sem=self.recv_sem.at[k],
            device_id=self.device(axis, off), device_id_type=pl.DeviceIdType.MESH)
        copy.start()
        self.sent.append(copy)
        return copy

    def put(self, src, dst):
        k = self.n_local
        self.n_local += 1
        copy = pltpu.make_async_copy(src, dst, self.local_sem.at[k])
        copy.start()
        self.local.append(copy)
        return copy

    def finish(self, waited=()):
        for copy in self.sent:
            copy.wait_send()
        for copy in self.local:
            if not any(copy is w for w in waited):
                copy.wait()


def gather_start(links, own, block, axis, pos):
    right = links.send(own, block(pos, None), axis, 1)
    left = links.send(own, block(pos, None), axis, -1)
    return right, left


def gather_forward(links, copies, block, axis, pos):
    copies[0].wait_recv()
    from_left = links.at(pos, -1)
    right = links.send(block(from_left, 0), block(from_left, 0), axis, 1)
    copies[1].wait_recv()
    from_right = links.at(pos, 1)
    left = links.send(block(from_right, 1), block(from_right, 1), axis, -1)
    return right, left


def gather_end(copies):
    for copy in copies:
        copy.wait_recv()


def dp_gather_start(links, own, slot):
    x, c = links.x, links.core
    block = lambda p, h: slot(2 * p + c, h)
    copies = gather_start(links, own, block, "x", x)
    mate = [links.send(own, slot(links.dp, None), "core")]
    return block, copies, mate


def dp_gather_forward(links, state):
    block, copies, mate = state
    x = links.x
    onward = gather_forward(links, copies, block, "x", x)
    for off in (-1, 1):
        b = block(links.at(x, off), None)
        mate.append(links.send(b, b, "core"))
    return block, onward, mate


def dp_gather_end(links, state):
    block, onward, mate = state
    far = links.at(links.x, 2)
    for h in (0, 1):
        onward[h].wait_recv()
        mate.append(links.send(block(far, h), block(far, h), "core"))
    return mate


def gather_kernel(x_ref, gy_ref, wg_ref, wu_ref, wd_ref,
                  xr_ref, gr_ref, xc_ref, gc_ref, wgf_ref, wuf_ref, wdf_ref,
                  send_sem, recv_sem, local_sem):
    links = Links(send_sem, recv_sem, local_sem)
    dp, z, y = links.dp, links.z, links.y
    links.barrier([("dp", o) for o in range(1, N_DP)] + [("z", 1), ("z", -1), ("y", 1), ("y", -1)])

    d_loc = wg_ref.shape[0]
    half_cols = x_ref.shape[1] // 2

    def row_slot(w_ref):
        rows = wg_ref.shape[0]

        def slot(j, h):
            if h is None:
                return w_ref.at[pl.ds(pl.multiple_of(j * rows, rows), rows)]
            return w_ref.at[pl.ds(pl.multiple_of(j * rows + h * (rows // 2), rows // 2), rows // 2)]
        return slot

    def col_slot(j, h):
        cols = pl.ds(pl.multiple_of(j * d_loc, d_loc), d_loc)
        rows = wd_ref.shape[0]
        if h is None:
            return wdf_ref.at[:, cols]
        return wdf_ref.at[pl.ds(h * (rows // 2), rows // 2), cols]

    def d_slice(ref, j):
        return ref.at[:, pl.ds(pl.multiple_of(j * d_loc, d_loc), d_loc)]

    def spread(src, dst):
        copies = [links.send(d_slice(src, (dp + o) % N_DP), dst.at[dp, z, y], "dp", o) for o in range(1, N_DP)]
        return copies, links.put(d_slice(src, dp), dst.at[dp, z, y])

    spread_x = spread(x_ref, xc_ref)
    spread_g = spread(gy_ref, gc_ref)

    def half(h):
        return pl.ds(h * half_cols, half_cols)

    def xr_first(p, h):
        return xr_ref.at[p, y] if h is None else xr_ref.at[p, y, :, half(h)]

    def xr_second(p, h):
        return xr_ref.at[:, p] if h is None else xr_ref.at[pl.ds(2 * h, 2), p]

    def gr_first(p, h):
        return gr_ref.at[z, p] if h is None else gr_ref.at[z, p, :, half(h)]

    def gr_second(p, h):
        return gr_ref.at[p] if h is None else gr_ref.at[p, pl.ds(2 * h, 2)]

    def dp_half(h):
        return pl.ds(h * (N_DP // 2), N_DP // 2)

    def xc_first(p, h):
        return xc_ref.at[:, p, y] if h is None else xc_ref.at[dp_half(h), p, y]

    def xc_second(p, h):
        return xc_ref.at[:, :, p] if h is None else xc_ref.at[dp_half(h), :, p]

    def gc_first(p, h):
        return gc_ref.at[:, z, p] if h is None else gc_ref.at[dp_half(h), z, p]

    def gc_second(p, h):
        return gc_ref.at[:, p] if h is None else gc_ref.at[dp_half(h), p]

    own_rows = [links.put(x_ref, xr_ref.at[z, y]), links.put(gy_ref, gr_ref.at[z, y])]
    xr = gather_start(links, x_ref, xr_first, "z", z)
    gr = gather_start(links, gy_ref, gr_first, "y", y)

    weights = [dp_gather_start(links, wg_ref, row_slot(wgf_ref)),
               dp_gather_start(links, wu_ref, row_slot(wuf_ref)),
               dp_gather_start(links, wd_ref, col_slot)]
    links.put(wg_ref, row_slot(wgf_ref)(dp, None))
    links.put(wu_ref, row_slot(wuf_ref)(dp, None))
    links.put(wd_ref, col_slot(dp, None))

    for copies, own in (spread_x, spread_g):
        for copy in copies:
            copy.wait_recv()
        own.wait()
    xc = gather_start(links, xc_first(z, None), xc_first, "z", z)
    gc = gather_start(links, gc_first(y, None), gc_first, "y", y)

    xr = gather_forward(links, xr, xr_first, "z", z)
    gr = gather_forward(links, gr, gr_first, "y", y)
    xc = gather_forward(links, xc, xc_first, "z", z)
    gc = gather_forward(links, gc, gc_first, "y", y)

    for copy in own_rows:
        copy.wait()
    gather_end(xr)
    xr = gather_start(links, xr_second(y, None), xr_second, "y", y)
    gather_end(gr)
    gr = gather_start(links, gr_second(z, None), gr_second, "z", z)
    gather_end(xc)
    xc = gather_start(links, xc_second(y, None), xc_second, "y", y)
    gather_end(gc)
    gc = gather_start(links, gc_second(z, None), gc_second, "z", z)

    weights[0] = dp_gather_forward(links, weights[0])
    xr = gather_forward(links, xr, xr_second, "y", y)
    gr = gather_forward(links, gr, gr_second, "z", z)
    xc = gather_forward(links, xc, xc_second, "y", y)
    gc = gather_forward(links, gc, gc_second, "z", z)
    weights[1] = dp_gather_forward(links, weights[1])
    weights[2] = dp_gather_forward(links, weights[2])

    for copies in (xr, gr, xc, gc):
        gather_end(copies)
    mates = [dp_gather_end(links, w) for w in weights]
    for mate in mates:
        gather_end(mate)
    links.finish(waited=[spread_x[1], spread_g[1]] + own_rows)


CHUNK = 1024


def add_into(dst, terms, write=None):
    lead, (rows, cols) = dst.shape[:-2], dst.shape[-2:]
    step = min(CHUNK, cols)
    for i in range(lead[0] if lead else 1):
        for c in range(0, cols, step):
            idx = ((i,) if lead else ()) + (slice(None), slice(c, c + step))
            total = terms[0][idx]
            for t in terms[1:]:
                total = total + t[idx]
            dst[idx] = total


def scatter_start(links, block, bufs, axis, pos):
    near0, near1, l_ref, r_ref, _, _ = bufs
    far = links.at(pos, 2)
    to_right = links.send(block(far, 0), near0, axis, 1)
    to_left = links.send(block(far, 1), near1, axis, -1)
    plain_r = links.send(block(links.at(pos, 1), 1), l_ref.at[1], axis, 1)
    plain_l = links.send(block(links.at(pos, -1), 0), r_ref.at[0], axis, -1)
    return to_right, to_left, plain_r, plain_l


def scatter_forward(links, state, block, bufs, axis, pos):
    near0, near1, l_ref, r_ref, stage_r, stage_l = bufs
    to_right, to_left, plain_r, plain_l = state
    to_right.wait_recv()
    add_into(stage_r, [block(links.at(pos, 1), 0), near0])
    sum_r = links.send(stage_r, l_ref.at[0], axis, 1)
    to_left.wait_recv()
    add_into(stage_l, [block(links.at(pos, -1), 1), near1])
    sum_l = links.send(stage_l, r_ref.at[1], axis, -1)
    return plain_r, plain_l, sum_r, sum_l


def exchange_kernel(h_ref, da_ref, db_ref, yp_ref, gp_ref, x_ref, gy_ref,
                    ha_ref, daa_ref, dba_ref, y_ref, gx_ref,
                    yn0, yn1, yl, yr, ysr, ysl, yres,
                    gn0, gn1, gl, gr, gsr, gsl, gres,
                    yn0b, yn1b, ylb, yrb, ysrb, yslb,
                    gn0b, gn1b, glb, grb, gsrb, gslb,
                    send_sem, recv_sem, local_sem):
    links = Links(send_sem, recv_sem, local_sem)
    dp, z, y = links.dp, links.z, links.y
    links.barrier([("x", 1), ("x", -1), ("core", 0), ("z", 1), ("z", -1), ("y", 1), ("y", -1)])

    rows = h_ref.shape[0]

    def row_slot(ref):
        def slot(j, h):
            if h is None:
                return ref.at[pl.ds(pl.multiple_of(j * rows, rows), rows)]
            return ref.at[pl.ds(pl.multiple_of(j * rows + h * (rows // 2), rows // 2), rows // 2)]
        return slot

    def y_first(p, h):
        return yp_ref.at[p, pl.ds(2 * h, 2)]

    def g_first(p, h):
        return gp_ref.at[pl.ds(2 * h, 2), p]

    half_cols = x_ref.shape[1] // 2

    def y_second(p, h):
        return yres.at[p, :, pl.ds(h * half_cols, half_cols)]

    def g_second(p, h):
        return gres.at[p, :, pl.ds(h * half_cols, half_cols)]

    yb1, gb1 = (yn0, yn1, yl, yr, ysr, ysl), (gn0, gn1, gl, gr, gsr, gsl)
    yb2, gb2 = (yn0b, yn1b, ylb, yrb, ysrb, yslb), (gn0b, gn1b, glb, grb, gsrb, gslb)

    ys = scatter_start(links, y_first, yb1, "z", z)
    gs = scatter_start(links, g_first, gb1, "y", y)
    refs = ((h_ref, ha_ref), (da_ref, daa_ref), (db_ref, dba_ref))
    acts = [dp_gather_start(links, src, row_slot(dst)) for src, dst in refs]
    for src, dst in refs:
        links.put(src, row_slot(dst)(dp, None))

    ys = scatter_forward(links, ys, y_first, yb1, "z", z)
    gs = scatter_forward(links, gs, g_first, gb1, "y", y)
    for i in range(3):
        acts[i] = dp_gather_forward(links, acts[i])

    gather_end(ys)
    for h in (0, 1):
        add_into(yres.at[pl.ds(2 * h, 2)], [y_first(z, h), yl.at[h], yr.at[h]])
    ys = scatter_start(links, y_second, yb2, "y", y)
    gather_end(gs)
    for h in (0, 1):
        add_into(gres.at[pl.ds(2 * h, 2)], [g_first(y, h), gl.at[h], gr.at[h]])
    gs = scatter_start(links, g_second, gb2, "z", z)
    ys = scatter_forward(links, ys, y_second, yb2, "y", y)
    gs = scatter_forward(links, gs, g_second, gb2, "z", z)

    mates = [dp_gather_end(links, acts[0])]
    gather_end(ys)
    gather_end(gs)
    step = min(CHUNK, half_cols)
    for own, second, pos, l_ref, r_ref, resid, out in (
            (yres, y_second, y, ylb, yrb, x_ref, y_ref), (gres, g_second, z, glb, grb, gy_ref, gx_ref)):
        for h in (0, 1):
            for c in range(0, half_cols, step):
                part = slice(c, c + step)
                both = slice(h * half_cols + c, h * half_cols + c + step)
                total = second(pos, h)[:, part] + l_ref[h, :, part] + r_ref[h, :, part]
                out[:, both] = (resid[:, both].astype(jnp.float32) + total).astype(out.dtype)

    mates += [dp_gather_end(links, acts[1]), dp_gather_end(links, acts[2])]
    for mate in mates:
        gather_end(mate)
    links.finish()


def solution(mesh):
    vmem = pl.BlockSpec(memory_space=VMEM)
    hbm = pl.BlockSpec(memory_space=pl.ANY)

    def local_step(x_loc, wg_loc, wu_loc, wd_loc, gy_loc):
        tok, d = x_loc.shape
        d_loc, ff = wg_loc.shape
        bf16, f32 = x_loc.dtype, jnp.float32
        sds = jax.ShapeDtypeStruct
        n_sem = 80
        xr, gr, xc, gc, wg, wu, wd = pl.pallas_call(
            gather_kernel,
            out_shape=[sds((RING, RING, tok, d), bf16), sds((RING, RING, tok, d), bf16),
                       sds((N_DP, RING, RING, tok, d_loc), bf16), sds((N_DP, RING, RING, tok, d_loc), bf16),
                       sds((d, ff), bf16), sds((d, ff), bf16), sds((ff, d), bf16)],
            in_specs=[vmem] * 5,
            out_specs=[hbm] * 7,
            scratch_shapes=[pltpu.SemaphoreType.DMA((n_sem,)), pltpu.SemaphoreType.DMA((n_sem,)),
                            pltpu.SemaphoreType.DMA((8,))],
            compiler_params=pltpu.CompilerParams(collective_id=0, has_side_effects=True),
            name="gather_all",
        )(x_loc, gy_loc, wg_loc, wu_loc, wd_loc)
        rows = RING * RING * tok
        x_rows, gy_rows = xr.reshape(rows, d), gr.reshape(rows, d)
        x_cols, gy_cols = xc.reshape(N_DP * rows, d_loc), gc.reshape(N_DP * rows, d_loc)

        gate_pre = jnp.dot(x_rows, wg, preferred_element_type=f32)
        up_pre = jnp.dot(x_rows, wu, preferred_element_type=f32)
        grad_h = jnp.einsum("nd,fd->nf", gy_rows, wd, preferred_element_type=f32)
        sig_gate = jax.nn.sigmoid(gate_pre)
        silu_gate = gate_pre * sig_gate
        hidden = (silu_gate * up_pre).astype(bf16)
        silu_deriv = sig_gate * (1.0 + gate_pre * (1.0 - sig_gate))
        grad_gate = (grad_h * up_pre * silu_deriv).astype(bf16)
        grad_up = (grad_h * silu_gate).astype(bf16)
        y_part = jnp.dot(hidden, wd, preferred_element_type=f32)
        gx_part = (jnp.einsum("nf,df->nd", grad_gate, wg, preferred_element_type=f32)
                   + jnp.einsum("nf,df->nd", grad_up, wu, preferred_element_type=f32))

        torus = (RING, RING, tok, d)
        half1, half2 = (2, tok, d), (tok, d // 2)
        first = [pltpu.VMEM(half1, f32)] * 2 + [pltpu.VMEM((2,) + half1, f32)] * 2 + [pltpu.VMEM(half1, f32)] * 2
        second = [pltpu.VMEM(half2, f32)] * 2 + [pltpu.VMEM((2,) + half2, f32)] * 2 + [pltpu.VMEM(half2, f32)] * 2
        res = [pltpu.VMEM((RING, tok, d), f32)]
        full = sds((N_DP * rows, ff), bf16)
        h_all, da_all, db_all, y_rows, gx_rows = pl.pallas_call(
            exchange_kernel,
            out_shape=[full, full, full, sds((tok, d), bf16), sds((tok, d), bf16)],
            in_specs=[vmem] * 7,
            out_specs=[hbm] * 3 + [vmem] * 2,
            scratch_shapes=first + res + first + res + second + second
            + [pltpu.SemaphoreType.DMA((n_sem,)), pltpu.SemaphoreType.DMA((n_sem,)), pltpu.SemaphoreType.DMA((8,))],
            compiler_params=pltpu.CompilerParams(collective_id=1, has_side_effects=True),
            name="exchange",
        )(hidden, grad_gate, grad_up, y_part.reshape(torus), gx_part.reshape(torus), x_loc, gy_loc)

        grad_wd = jnp.einsum("nf,nd->fd", h_all, gy_cols, preferred_element_type=f32)
        grad_wg = jnp.einsum("nd,nf->df", x_cols, da_all, preferred_element_type=f32)
        grad_wu = jnp.einsum("nd,nf->df", x_cols, db_all, preferred_element_type=f32)
        return y_rows, gx_rows, grad_wg, grad_wu, grad_wd

    row_spec = P(("dp", "tp"), None)
    up_spec = P("dp", "tp")
    down_spec = P("tp", "dp")
    return jax.shard_map(local_step, mesh=mesh,
                         in_specs=(row_spec, up_spec, up_spec, down_spec, row_spec),
                         out_specs=(row_spec, row_spec, up_spec, up_spec, down_spec),
                         check_vma=False)
```

time: 565 us -> 228 us (0.40)
  waiting for transfers between devices: 441 us -> 0 us
  Pallas kernels: 0 us -> 182 us
  blocking collectives: 19.3 us -> 0 us
  local copies, waits for them, and re-layouts: 15.4 us -> 1.85 us
  between operations: 13.9 us -> 0.81 us
  matrix products: 55.6 us -> 43.5 us
  starting transfers between devices: 10.4 us -> 0 us
  other arithmetic: 8.36 us -> 0.01 us
    pallas_call x0 -> x2, Pallas kernels: none -> 182 us  [the longest x1 118 us: local_step(): pl.pallas_call(gather_kernel, out_shape=[sds((RING, RING, tok, d), bf16),...]
    all_gather x5 -> x0, waiting for transfers between devices: 158 us -> none  [the longest x2 72.9 us: spread_cols(): gathered = lax.all_gather(cols_mine, 'tp', axis=1)]
    reduce_scatter x3 -> x0, waiting for transfers between devices: 150 us -> none  [the longest x1 54.5 us: local_step(): lax.psum_scatter(jnp.dot(x_cols, wu_loc, preferred_element_type=jnp.float...]
    unnamed x10 -> x0, waiting for transfers between devices: 130 us -> none
    all_to_all x2 -> x0, blocking collectives: 19.3 us -> none  [spread_cols(): cols_mine = lax.all_to_all(rows_loc, 'dp', 1, 0, tiled=True)]
    dot_general x9, matrix products: 55.6 us -> 43.5 us  [the longest x1 8.28 us: local_step(): y_part = jnp.dot(hidden, wd, preferred_element_type=f32)]
    all_to_all x2 -> x0, starting transfers between devices: 9.86 us -> none  [collect_rows(): lax.all_to_all(summed.astype(jnp.bfloat16), 'dp', 0, 2, tiled=True)]
    convert_element_type x3 -> x0, other arithmetic: 8.36 us -> none  [the longest x2 4.52 us: collect_rows(): summed.astype(jnp.bfloat16)]
  transfers between devices with their start and end apart: 11 -> 0, of which waited for: 10 -> 0; matrix products, arithmetic and copies ran while one was open for 11% -> 0% of each run, Pallas kernels for 0% -> 0%
where the time goes in v1:
time: 228 us
  Pallas kernels  182 us (80%)
  matrix products  43.5 us (19%)
    pallas_call x1, Pallas kernels, local_step(): pl.pallas_call(gather_kernel, out_shape=[sds((RING, RING, tok, d), bf16),...  118 us
    pallas_call x1, Pallas kernels, local_step(): pl.pallas_call(exchange_kernel, out_shape=[full, full, full, sds((tok, d)...  63.3 us
    dot_general x1, matrix products, local_step(): y_part = jnp.dot(hidden, wd, preferred_element_type=f32)  8.28 us
    dot_general x1, matrix products, local_step(): up_pre = jnp.dot(x_rows, wu, preferred_element_type=f32)  6.48 us
    dot_general x1, matrix products, local_step(): grad_h = jnp.einsum('nd,fd->nf', gy_rows, wd, preferred_element_type=f32)  6.1 us
    dot_general x1, matrix products, local_step(): jnp.einsum('nf,nd->fd', h_all, gy_cols, preferred_element_type=f32)  6.02 us

profile of v1, /device:TPU:1, one launch (start us, length us, event | category | flops | bytes accessed | tf_op | source)
XLA Modules:
  0.0 227.7 jit_solution(7897823404733774474)
XLA Ops:
  0.6 118.3 %gather_all.1 = (bf16[4,4,16,4096]{3,2,1,0:T(8,128)(2,1)}, bf16[4,4,16,4096]{3,2,1,0:T(8,128)(2,1)}, bf16[8,4,4,16,512]{4,3,2,1,0:T(8,128)(2,1)}, bf16[8,4,4,16,...) custom-call(bf16[16,4096]{1,0:T(8,128)(2,1)} %x_ref.3, ...), custom_call_target="tpu_custom_call" | custom-call | tf_op jit(solution)/shard_map/gather_all/pallas_call | solution.py:360
  118.9 0.0 copy-start.6
  118.9 0.0 copy-start.11
  119.0 6.5 %fusion.2 = f32[256,1024]{1,0:T(8,128)S(1)} fusion(bf16[256,4096]{1,0:T(8,128)(2,1)} %bitcast.32, bf16[4096,1024]{1,0:T(8,128)(2,1)} %get-tuple-element.19), kind=kOutput, calls=%fused_computation.7 | convolution fusion | flops 2147483648 | bytes 11534336 | tf_op jit(solution)/shard_map/dot_general | solution.py:377
  125.4 0.0 copy-done.6
  125.5 0.5 copy-done.11
  125.9 2.4 %fusion.1 = f32[256,1024]{1,0:T(8,128)S(1)} fusion(bf16[256,4096]{1,0:T(8,128)(2,1)S(1)} %bitcast.33, bf16[4096,1024]{1,0:T(8,128)(2,1)S(1)} %copy-done.6), kind=kOutput, calls=%fused_computation.6 | convolution fusion | flops 2147483648 | bytes 11534336 | tf_op jit(solution)/shard_map/dot_general | solution.py:376
  128.3 0.0 copy-done.10
  128.3 6.1 %multiply_convert_fusion = (bf16[256,1024]{1,0:T(8,128)(2,1)S(1)}, bf16[256,1024]{1,0:T(8,128)(2,1)S(1)}, bf16[256,1024]{1,0:T(8,128)(2,1)S(1)}) fusion(f32[256,1024]{1,0:T(8,128)S(1)} %fusion.1, f32[256,1024]{1,0:T(8,128)S(1)} %fusion.2, bf16[256,4096]{1,0:T(8,128)(2,1)S(1)} %bitcast.31, bf16[1024,4096]{1,0:T(8,128)(2,1)} %get-tuple-element.21), kind=kOutput, calls=%fused_computation.1 | convolution fusion | flops 2151415808 | bytes 14155776 | tf_op jit(solution)/shard_map/nd,fd->nf/dot_general | solution.py:378
  134.4 0.0 copy-start.3
  134.4 0.0 copy-start.2
  134.4 0.0 copy-start.1
  134.5 0.0 slice-start
  134.5 8.3 %fusion.3 = f32[256,4096]{1,0:T(8,128)} fusion(bf16[256,1024]{1,0:T(8,128)(2,1)S(1)} %get-tuple-element.31.h_ref, bf16[1024,4096]{1,0:T(8,128)(2,1)} %get-tuple-element.21), kind=kOutput, calls=%fused_computation.8 | convolution fusion | flops 2147483648 | bytes 13107200 | tf_op jit(solution)/shard_map/dot_general | solution.py:385
  142.8 0.0 copy-done.3
  142.8 0.0 copy-done.2
  142.8 2.4 %fusion.4 = f32[256,4096]{1,0:T(8,128)S(1)} fusion(bf16[256,1024]{1,0:T(8,128)(2,1)S(1)} %get-tuple-element.30.da_ref, bf16[4096,1024]{1,0:T(8,128)(2,1)S(1)} %copy-done.6), kind=kOutput, calls=%fused_computation.9 | convolution fusion | flops 2147483648 | bytes 13107200 | tf_op jit(solution)/shard_map/nf,df->nd/dot_general | solution.py:386
  145.2 0.0 copy-done.1
  145.2 0.0 slice-done
  145.2 0.0 slice-done.1
  145.2 4.5 %convolution_add_fusion = f32[256,4096]{1,0:T(8,128)} fusion(f32[256,4096]{1,0:T(8,128)S(1)} %fusion.4, bf16[256,1024]{1,0:T(8,128)(2,1)S(1)} %get-tuple-element.29.db_ref, bf16[4096,1024]{1,0:T(8,128)(2,1)S(1)} %bitcast.28), kind=kOutput, calls=%fused_computation | convolution fusion | flops 2148532224 | bytes 17301504 | tf_op jit(solution)/shard_map/nf,df->nd/dot_general | solution.py:387
  149.7 63.3 %exchange.1 = (bf16[2048,1024]{1,0:T(8,128)(2,1)}, bf16[2048,1024]{1,0:T(8,128)(2,1)}, bf16[2048,1024]{1,0:T(8,128)(2,1)}, bf16[16,4096]{1,0:T(8,128)(2,1)}, bf16[16,4096]{1,0:T(8,128)(2,1)}) custom-call(bf16[256,1024]{1,0:T(8,128)(2,1)} %copy-done.3, bf16[256,1024]{1,0:T(8,128)(2,1)} %copy-done.2, bf16[256,1024]{1,0:T(8,128)(2,1)} %copy-done.1, ...), custom_call_target="tpu_custom_call" | custom-call | tf_op jit(solution)/shard_map/exchange/pallas_call | solution.py:395
  213.0 0.0 copy-done
  213.0 0.0 copy-start.8
  213.0 0.0 copy-start.9
  213.0 6.0 %fusion.7 = f32[1024,512]{1,0:T(8,128)} fusion(bf16[2048,1024]{1,0:T(8,128)(2,1)} %get-tuple-element.27, bf16[2048,512]{1,0:T(8,128)(2,1)S(1)} %bitcast.26), kind=kOutput, calls=%fused_computation.12 | convolution fusion | flops 2147483648 | bytes 8388608 | tf_op jit(solution)/shard_map/nf,nd->fd/dot_general | solution.py:406
  219.1 3.7 %fusion.5 = f32[512,1024]{1,0:T(8,128)} fusion(bf16[2048,512]{1,0:T(8,128)(2,1)S(1)} %bitcast.29, bf16[2048,1024]{1,0:T(8,128)(2,1)S(1)} %copy-done.8), kind=kOutput, calls=%fused_computation.10 | convolution fusion | flops 2147483648 | bytes 8388608 | tf_op jit(solution)/shard_map/nd,nf->df/dot_general | solution.py:407
  222.7 0.0 copy-done.7
  222.7 3.7 %fusion.6 = f32[512,1024]{1,0:T(8,128)} fusion(bf16[2048,512]{1,0:T(8,128)(2,1)S(1)} %bitcast.30, bf16[2048,1024]{1,0:T(8,128)(2,1)S(1)} %copy-done.7), kind=kOutput, calls=%fused_computation.11 | convolution fusion | flops 2147483648 | bytes 8388608 | tf_op jit(solution)/shard_map/nd,nf->df/dot_general | solution.py:408
  226.4 0.7 copy.12
  227.1 0.0 copy-done.4
  227.1 0.7 copy.13
  (10 shorter events, 0.0 us)
Async XLA Ops:
  118.9 6.5 %copy-start.6 = (bf16[4096,1024]{1,0:T(8,128)(2,1)S(1)}, bf16[4096,1024]{1,0:T(8,128)(2,1)}, u32[]{:S(2)}) copy-start(bf16[4096,1024]{1,0:T(8,128)(2,1)} %get-tuple-element.18) | copy-start | bytes 25165828
  118.9 7.0 %copy-start.11 = (bf16[4,4,16,4096]{3,2,1,0:T(8,128)(2,1)S(1)}, bf16[4,4,16,4096]{3,2,1,0:T(8,128)(2,1)}, u32[]{:S(2)}) copy-start(bf16[4,4,16,4096]{3,2,1,0:T(8,128)(2,1)} %get-tuple-element.17) | copy-start | bytes 6291460
  125.9 2.4 %copy-start.10 = (bf16[4,4,16,4096]{3,2,1,0:T(8,128)(2,1)S(1)}, bf16[4,4,16,4096]{3,2,1,0:T(8,128)(2,1)}, u32[]{:S(2)}) copy-start(bf16[4,4,16,4096]{3,2,1,0:T(8,128)(2,1)} %get-tuple-element.20) | copy-start | bytes 6291460
  134.4 8.3 %copy-start.3 = (bf16[256,1024]{1,0:T(8,128)(2,1)}, bf16[256,1024]{1,0:T(8,128)(2,1)S(1)}, u32[]{:S(2)}) copy-start(bf16[256,1024]{1,0:T(8,128)(2,1)S(1)} %get-tuple-element.31.h_ref) | copy-start | bytes 1572868
  134.4 8.3 %copy-start.2 = (bf16[256,1024]{1,0:T(8,128)(2,1)}, bf16[256,1024]{1,0:T(8,128)(2,1)S(1)}, u32[]{:S(2)}) copy-start(bf16[256,1024]{1,0:T(8,128)(2,1)S(1)} %get-tuple-element.30.da_ref) | copy-start | bytes 1572868
  134.4 10.7 %copy-start.1 = (bf16[256,1024]{1,0:T(8,128)(2,1)}, bf16[256,1024]{1,0:T(8,128)(2,1)S(1)}, u32[]{:S(2)}) copy-start(bf16[256,1024]{1,0:T(8,128)(2,1)S(1)} %get-tuple-element.29.db_ref) | copy-start | bytes 1572868
  134.5 10.7 %slice-start = ((s8[8388608]{0:T(1024)(128)(4,1)}), s8[4194304]{0:T(1024)(128)(4,1)S(1)}, s32[]{:S(2)}) async-start(s8[8388608]{0:T(1024)(128)(4,1)} %bitcast.27), calls=%async_computation | async-start | bytes 8388608
  142.8 2.4 %slice-start.1 = ((s8[8388608]{0:T(1024)(128)(4,1)}), s8[4194304]{0:T(1024)(128)(4,1)S(1)}, s32[]{:S(2)}) async-start(s8[8388608]{0:T(1024)(128)(4,1)} %bitcast.27), calls=%async_computation.1 | async-start | bytes 8388608
  149.7 63.3 %copy-start = (bf16[8,4,4,16,512]{4,3,2,1,0:T(8,128)(2,1)S(1)}, bf16[8,4,4,16,512]{4,3,2,1,0:T(8,128)(2,1)}, u32[]{:S(2)}) copy-start(bf16[8,4,4,16,512]{4,3,2,1,0:T(8,128)(2,1)} %get-tuple-element.28) | copy-start | bytes 6291460
  213.0 6.0 %copy-start.8 = (bf16[2048,1024]{1,0:T(8,128)(2,1)S(1)}, bf16[2048,1024]{1,0:T(8,128)(2,1)}, u32[]{:S(2)}) copy-start(bf16[2048,1024]{1,0:T(8,128)(2,1)} %get-tuple-element.25) | copy-start | bytes 12582916
  213.0 6.0 %copy-start.9 = (bf16[8,4,4,16,512]{4,3,2,1,0:T(8,128)(2,1)S(1)}, bf16[8,4,4,16,512]{4,3,2,1,0:T(8,128)(2,1)}, u32[]{:S(2)}) copy-start(bf16[8,4,4,16,512]{4,3,2,1,0:T(8,128)(2,1)} %get-tuple-element.24) | copy-start | bytes 6291460
  219.1 3.7 %copy-start.7 = (bf16[2048,1024]{1,0:T(8,128)(2,1)S(1)}, bf16[2048,1024]{1,0:T(8,128)(2,1)}, u32[]{:S(2)}) copy-start(bf16[2048,1024]{1,0:T(8,128)(2,1)} %get-tuple-element.26) | copy-start | bytes 12582916
  222.7 3.7 %copy-start.5 = (bf16[16,4096]{1,0:T(8,128)(2,1)S(1)}, bf16[16,4096]{1,0:T(8,128)(2,1)}, u32[]{:S(2)}) copy-start(bf16[16,4096]{1,0:T(8,128)(2,1)} %get-tuple-element.37) | copy-start | bytes 393220
  222.7 4.3 %copy-start.4 = (bf16[16,4096]{1,0:T(8,128)(2,1)S(1)}, bf16[16,4096]{1,0:T(8,128)(2,1)}, u32[]{:S(2)}) copy-start(bf16[16,4096]{1,0:T(8,128)(2,1)} %get-tuple-element.38) | copy-start | bytes 393220

commit v2 on v0

v2 whole, which is shorter than its diff:
```python
import jax
import jax.numpy as jnp
from jax import lax
from jax.experimental import pallas as pl
from jax.experimental.pallas import tpu as pltpu
from jax.sharding import PartitionSpec as P

RING = 4
N_DP = 2 * RING
VMEM = pltpu.MemorySpace.VMEM


class Links:
    def __init__(self, send_sem, recv_sem, local_sem):
        self.send_sem, self.recv_sem, self.local_sem = send_sem, recv_sem, local_sem
        self.n_remote = self.n_local = 0
        self.sent, self.local = [], []
        dp, tp = lax.axis_index("dp"), lax.axis_index("tp")
        self.dp, self.tp = dp, tp
        self.x, self.core = dp // 2, dp % 2
        self.z, self.y = tp // RING, tp % RING

    def at(self, pos, off):
        return (pos + off) % RING

    def device(self, axis, off):
        if axis == "x":
            return {"dp": 2 * self.at(self.x, off) + self.core, "tp": self.tp}
        if axis == "core":
            return {"dp": 2 * self.x + (1 - self.core), "tp": self.tp}
        if axis == "dp":
            return {"dp": (self.dp + off) % N_DP, "tp": self.tp}
        if axis == "z":
            return {"dp": self.dp, "tp": RING * self.at(self.z, off) + self.y}
        return {"dp": self.dp, "tp": RING * self.z + self.at(self.y, off)}

    def barrier(self, peers):
        sem = pltpu.get_barrier_semaphore()
        for axis, off in peers:
            pl.semaphore_signal(sem, inc=1, device_id=self.device(axis, off),
                                device_id_type=pl.DeviceIdType.MESH)
        pl.semaphore_wait(sem, len(peers))

    def send(self, src, dst, axis, off=0):
        k = self.n_remote
        self.n_remote += 1
        copy = pltpu.make_async_remote_copy(
            src_ref=src, dst_ref=dst, send_sem=self.send_sem.at[k], recv_sem=self.recv_sem.at[k],
            device_id=self.device(axis, off), device_id_type=pl.DeviceIdType.MESH)
        copy.start()
        self.sent.append(copy)
        return copy

    def put(self, src, dst):
        k = self.n_local
        self.n_local += 1
        copy = pltpu.make_async_copy(src, dst, self.local_sem.at[k])
        copy.start()
        self.local.append(copy)
        return copy

    def sent_all(self):
        for copy in self.sent:
            copy.wait_send()
        self.sent = []

    def put_all(self):
        for copy in self.local:
            copy.wait()
        self.local = []


def gather_start(links, own, block, axis, pos):
    right = links.send(own, block(pos, None), axis, 1)
    left = links.send(own, block(pos, None), axis, -1)
    return right, left


def gather_forward(links, copies, block, axis, pos):
    copies[0].wait_recv()
    from_left = links.at(pos, -1)
    right = links.send(block(from_left, 0), block(from_left, 0), axis, 1)
    copies[1].wait_recv()
    from_right = links.at(pos, 1)
    left = links.send(block(from_right, 1), block(from_right, 1), axis, -1)
    return right, left


def gather_end(copies):
    for copy in copies:
        copy.wait_recv()


class DpGather:
    def __init__(self, links, own, slot):
        self.links, self.slot = links, slot
        x, c = links.x, links.core
        self.block = lambda p, h: slot(2 * p + c, h)
        self.ring = gather_start(links, own, self.block, "x", x)
        self.mate = [links.send(own, slot(links.dp, None), "core")]

    def forward(self):
        links = self.links
        self.ring = gather_forward(links, self.ring, self.block, "x", links.x)
        for off in (-1, 1):
            b = self.block(links.at(links.x, off), None)
            self.mate.append(links.send(b, b, "core"))

    def near(self):
        gather_end(self.mate)
        self.mate = []

    def far(self):
        links = self.links
        far = links.at(links.x, 2)
        for h in (0, 1):
            self.ring[h].wait_recv()
            b = self.block(far, h)
            self.mate.append(links.send(b, b, "core"))


class Scatter:
    def __init__(self, links, part, cols, z_first, bufs):
        self.links, z, y = links, links.z, links.y
        lo, width = cols
        half = width // 2
        self.half = half
        both = pl.ds(lo, width)
        if z_first:
            self.axes, self.pos = ("z", "y"), (z, y)
            first = lambda p, h: part.at[p, pl.ds(2 * h, 2), :, both]
            second = lambda p, h: part.at[z, p, :, pl.ds(lo + h * half, half)]
        else:
            self.axes, self.pos = ("y", "z"), (y, z)
            first = lambda p, h: part.at[pl.ds(2 * h, 2), p, :, both]
            second = lambda p, h: part.at[p, y, :, pl.ds(lo + h * half, half)]
        self.block = (first, second)
        self.bufs = (bufs[:4], bufs[4:])

    def start(self, phase):
        links, block, axis, pos = self.links, self.block[phase], self.axes[phase], self.pos[phase]
        near0, near1, l_ref, r_ref = self.bufs[phase]
        far = links.at(pos, 2)
        self.first = (links.send(block(far, 0), near0, axis, 1), links.send(block(far, 1), near1, axis, -1))
        self.last = [links.send(block(links.at(pos, 1), 1), l_ref.at[1], axis, 1),
                     links.send(block(links.at(pos, -1), 0), r_ref.at[0], axis, -1)]

    def forward(self, phase):
        links, block, axis, pos = self.links, self.block[phase], self.axes[phase], self.pos[phase]
        near0, near1, l_ref, r_ref = self.bufs[phase]
        for copy, off, h, near, dst in ((self.first[0], 1, 0, near0, l_ref), (self.first[1], -1, 1, near1, r_ref)):
            copy.wait_recv()
            b = block(links.at(pos, off), h)
            add_into(b, [near])
            self.last.append(links.send(b, dst.at[h], axis, off))

    def end(self, phase):
        block, pos = self.block[phase], self.pos[phase]
        _, _, l_ref, r_ref = self.bufs[phase]
        gather_end(self.last)
        for h in (0, 1):
            add_into(block(pos, h), [l_ref.at[h], r_ref.at[h]])

    def result(self, h):
        return self.block[1](self.pos[1], h)


CHUNK = 1024
TILE = 256


def add_into(dst, terms):
    lead, cols = dst.shape[:-2], dst.shape[-1]
    step = min(CHUNK, cols)
    for i in range(lead[0] if lead else 1):
        for c in range(0, cols, step):
            idx = ((i,) if lead else ()) + (slice(None), slice(c, c + step))
            total = dst[idx]
            for t in terms:
                total = total + t[idx]
            dst[idx] = total


def loop(n, body):
    def step(i, carry):
        body(i)
        return carry
    lax.fori_loop(0, n, step, 0)


def part_of(i, size):
    return pl.ds(pl.multiple_of(i * size, size), size)


NN = (((1,), (0,)), ((), ()))
NT = (((1,), (1,)), ((), ()))
TN = (((0,), (0,)), ((), ()))


def dot(a, b, dims):
    return lax.dot_general(a, b, dims, preferred_element_type=jnp.float32)


def mlp_kernel(x_ref, gy_ref, wg_ref, wu_ref, wd_ref,
               y_ref, gx_ref, gwg_ref, gwu_ref, gwd_ref, xc_ref, gc_ref,
               wgf, wuf, wdf, xr, gr, ha, daa, dba, acc_g, acc_u, acc_d, y_part, gx_part, *rest):
    scat_bufs, (send_sem, recv_sem, local_sem) = rest[:-3], rest[-3:]
    links = Links(send_sem, recv_sem, local_sem)
    dp, z, y, x = links.dp, links.z, links.y, links.x
    tok, d = x_ref.shape
    d_loc, ff = wg_ref.shape
    rows = RING * RING * tok
    bf16 = x_ref.dtype
    links.barrier([("dp", o) for o in range(1, N_DP)] + [("z", 1), ("z", -1), ("y", 1), ("y", -1)])

    def row_slot(ref, n):
        def slot(j, h):
            if h is None:
                return ref.at[part_of(j, n)]
            return ref.at[part_of(2 * j + h, n // 2)]
        return slot

    def col_slot(j, h):
        if h is None:
            return wdf.at[:, part_of(j, d_loc)]
        return wdf.at[pl.ds(h * (ff // 2), ff // 2), part_of(j, d_loc)]

    def spread(src, dst):
        def d_slice(j):
            return src.at[:, part_of(j, d_loc)]
        return ([links.send(d_slice((dp + o) % N_DP), dst.at[dp, z, y], "dp", o) for o in range(1, N_DP)],
                links.put(d_slice(dp), dst.at[dp, z, y]))

    spread_x = spread(x_ref, xc_ref)
    spread_g = spread(gy_ref, gc_ref)

    def row_half(h):
        return pl.ds(h * (d // 2), d // 2)

    def dp_half(h):
        return pl.ds(h * (N_DP // 2), N_DP // 2)

    def xr_first(p, h):
        return xr.at[p, y] if h is None else xr.at[p, y, :, row_half(h)]

    def xr_second(p, h):
        return xr.at[:, p] if h is None else xr.at[pl.ds(2 * h, 2), p]

    def gr_first(p, h):
        return gr.at[z, p] if h is None else gr.at[z, p, :, row_half(h)]

    def gr_second(p, h):
        return gr.at[p] if h is None else gr.at[p, pl.ds(2 * h, 2)]

    def xc_first(p, h):
        return xc_ref.at[:, p, y] if h is None else xc_ref.at[dp_half(h), p, y]

    def xc_second(p, h):
        return xc_ref.at[:, :, p] if h is None else xc_ref.at[dp_half(h), :, p]

    def gc_first(p, h):
        return gc_ref.at[:, z, p] if h is None else gc_ref.at[dp_half(h), z, p]

    def gc_second(p, h):
        return gc_ref.at[:, p] if h is None else gc_ref.at[dp_half(h), p]

    links.put(x_ref, xr.at[z, y])
    links.put(gy_ref, gr.at[z, y])
    rx = gather_start(links, x_ref, xr_first, "z", z)
    rg = gather_start(links, gy_ref, gr_first, "y", y)

    gate = DpGather(links, wg_ref, row_slot(wgf, d_loc))
    up = DpGather(links, wu_ref, row_slot(wuf, d_loc))
    down = DpGather(links, wd_ref, col_slot)
    links.put(wg_ref, wgf.at[part_of(dp, d_loc)])
    links.put(wu_ref, wuf.at[part_of(dp, d_loc)])
    links.put(wd_ref, wdf.at[:, part_of(dp, d_loc)])

    gather_end(spread_x[0])
    gather_end(spread_g[0])
    links.put_all()
    cx = gather_start(links, xc_first(z, None), xc_first, "z", z)
    cg = gather_start(links, gc_first(y, None), gc_first, "y", y)

    rx = gather_forward(links, rx, xr_first, "z", z)
    rg = gather_forward(links, rg, gr_first, "y", y)
    cx = gather_forward(links, cx, xc_first, "z", z)
    cg = gather_forward(links, cg, gc_first, "y", y)
    gather_end(rx)
    rx = gather_start(links, xr_second(y, None), xr_second, "y", y)
    gather_end(rg)
    rg = gather_start(links, gr_second(z, None), gr_second, "z", z)
    gather_end(cx)
    cx = gather_start(links, xc_second(y, None), xc_second, "y", y)
    gather_end(cg)
    cg = gather_start(links, gc_second(z, None), gc_second, "z", z)
    gate.forward()
    rx = gather_forward(links, rx, xr_second, "y", y)
    rg = gather_forward(links, rg, gr_second, "z", z)
    cx = gather_forward(links, cx, xc_second, "y", y)
    cg = gather_forward(links, cg, gc_second, "z", z)
    for copies in (rx, rg, cx, cg):
        gather_end(copies)

    a_acc, b_acc, g_acc = acc_g.at[pl.ds(0, rows)], acc_g.at[pl.ds(rows, rows)], acc_u.at[pl.ds(0, rows)]
    ff_tile = min(TILE, ff)
    n_ff = ff // ff_tile
    d_tile = min(TILE, d_loc)
    n_d = d_loc // d_tile

    def near_block(i):
        q = i // 2
        return 2 * ((x + q + q // 2) % RING) + i % 2

    def far_block(i):
        return 2 * ((x + 2) % RING) + i % 2

    def cols_of(ref, j):
        return ref[:, :, :, part_of(j, d_loc)].reshape(rows, d_loc)

    def clear(*refs):
        for ref in refs:
            n, step = ref.shape[0], min(16, ref.shape[0])

            def body(i):
                ref[part_of(i, step)] = jnp.zeros((step, ref.shape[1]), jnp.float32)
            loop(n // step, body)

    def add_up_side(acc, w, src, block, n):
        def body(i):
            j, t = block(i // n_ff), part_of(i % n_ff, ff_tile)
            acc[:, t] += dot(cols_of(src, j), w[part_of(j, d_loc), t], NN)
        loop(n * n_ff, body)

    def add_down_side(block, n):
        def body(i):
            j, t = block(i // n_ff), part_of(i % n_ff, ff_tile)
            g_acc[:, t] += dot(cols_of(gr, j), wdf[t, part_of(j, d_loc)], NT)
        loop(n * n_ff, body)

    clear(acc_g, acc_u)
    up.forward()
    gate.near()
    add_up_side(a_acc, wgf, xr, near_block, 6)
    up.near()
    add_up_side(b_acc, wuf, xr, near_block, 6)
    down.forward()
    down.near()
    add_down_side(near_block, 6)

    gate.far()
    gate.near()
    add_up_side(a_acc, wgf, xr, far_block, 2)
    up.far()
    up.near()
    add_up_side(b_acc, wuf, xr, far_block, 2)

    step_rows = 16

    def hidden_step(i):
        r = part_of(i, step_rows)
        a = a_acc[r]
        ha[part_of(dp * (rows // step_rows) + i, step_rows)] = (a * jax.nn.sigmoid(a) * b_acc[r]).astype(bf16)

    loop(rows // step_rows, hidden_step)
    hid = DpGather(links, ha.at[part_of(dp, rows)], row_slot(ha, rows))

    def y_block(block, n):
        def body(i):
            t = part_of(block(i // n_d) * n_d + i % n_d, d_tile)
            y_part[:, :, :, t] = dot(ha[part_of(dp, rows)], wdf[:, t], NN).reshape(RING, RING, tok, d_tile)
        loop(n * n_d, body)

    y_block(near_block, 6)
    down.far()
    down.near()
    add_down_side(far_block, 2)

    def grad_step(i):
        r = part_of(i, step_rows)
        own = part_of(dp * (rows // step_rows) + i, step_rows)
        a, b, g = a_acc[r], b_acc[r], g_acc[r]
        s = jax.nn.sigmoid(a)
        daa[own] = (g * b * (s * (1.0 + a * (1.0 - s)))).astype(bf16)
        dba[own] = (g * (a * s)).astype(bf16)

    loop(rows // step_rows, grad_step)
    dgate = DpGather(links, daa.at[part_of(dp, rows)], row_slot(daa, rows))
    dup = DpGather(links, dba.at[part_of(dp, rows)], row_slot(dba, rows))

    y_block(far_block, 2)
    n_buf = len(scat_bufs) // 4
    half = d // 2
    bufs = [scat_bufs[k * n_buf:(k + 1) * n_buf] for k in range(4)]
    ys = [Scatter(links, y_part, (0, half), True, bufs[0]), Scatter(links, y_part, (half, half), False, bufs[1])]
    gs = [Scatter(links, gx_part, (0, half), True, bufs[2]), Scatter(links, gx_part, (half, half), False, bufs[3])]
    for s in ys:
        s.start(0)

    def gx_step(i):
        t = part_of(i, d_tile)
        own = part_of(dp, rows)
        gx_part[:, :, :, t] = (dot(daa[own], wgf[t], NT) + dot(dba[own], wuf[t], NT)).reshape(RING, RING, tok, d_tile)

    n_half = half // d_tile
    loop(n_half, gx_step)
    for s in ys:
        s.forward(0)
    gs[0].start(0)
    loop(n_half, lambda i: gx_step(i + n_half))
    gs[1].start(0)

    links.sent_all()
    for j in range(N_DP):
        links.put(xc_ref.at[j], xr.at[:, :, :, pl.ds(j * d_loc, d_loc)])
        links.put(gc_ref.at[j], gr.at[:, :, :, pl.ds(j * d_loc, d_loc)])
    clear(acc_g, acc_u, acc_d)

    def add_wd(block, n):
        def body(i):
            j, t = block(i // n_ff), part_of(i % n_ff, ff_tile)
            acc_d[t] += dot(ha[part_of(j, rows), t], cols_of(gr, j), TN)
        loop(n * n_ff, body)

    def add_wup(acc, src, block, n):
        def body(i):
            j, t = block(i // n_ff), part_of(i % n_ff, ff_tile)
            acc[pl.ds(0, d_loc), t] += dot(cols_of(xr, j), src[part_of(j, rows), t], TN)
        loop(n * n_ff, body)

    hid.forward()
    for s in gs:
        s.forward(0)
    for s in ys:
        s.end(0)
        s.start(1)
    dgate.forward()
    for s in ys:
        s.forward(1)
    links.put_all()
    hid.near()
    add_wd(near_block, 6)

    def finish_rows(units, resid, out):
        for s, lo in zip(units, (0, half)):
            s.end(1)
            for h in (0, 1):
                step = min(CHUNK, s.half)
                for c in range(0, s.half, step):
                    cols = slice(lo + h * s.half + c, lo + h * s.half + c + step)
                    total = resid[:, cols].astype(jnp.float32) + s.result(h)[:, c:c + step]
                    out[:, cols] = total.astype(out.dtype)

    finish_rows(ys, x_ref, y_ref)
    dup.forward()
    for s in gs:
        s.end(0)
        s.start(1)
    dgate.near()
    add_wup(acc_g, daa, near_block, 6)
    hid.far()
    for s in gs:
        s.forward(1)
    hid.near()
    add_wd(far_block, 2)
    links.put(acc_d, gwd_ref)
    dup.near()
    add_wup(acc_u, dba, near_block, 6)
    dgate.far()
    finish_rows(gs, gy_ref, gx_ref)
    dgate.near()
    add_wup(acc_g, daa, far_block, 2)
    links.put(acc_g.at[pl.ds(0, d_loc)], gwg_ref)
    dup.far()
    dup.near()
    add_wup(acc_u, dba, far_block, 2)
    links.put(acc_u.at[pl.ds(0, d_loc)], gwu_ref)
    links.sent_all()
    links.put_all()


def solution(mesh):
    vmem = pl.BlockSpec(memory_space=VMEM)
    hbm = pl.BlockSpec(memory_space=pl.ANY)

    def local_step(x_loc, wg_loc, wu_loc, wd_loc, gy_loc):
        tok, d = x_loc.shape
        d_loc, ff = wg_loc.shape
        bf16, f32 = x_loc.dtype, jnp.float32
        sds = jax.ShapeDtypeStruct
        n_sem = 160
        rows = RING * RING * tok
        spread = sds((N_DP, RING, RING, tok, d_loc), bf16)
        up_rows = max(d_loc, 2 * rows)
        whole = pltpu.VMEM((N_DP * rows, ff), bf16)
        half1, half2 = (2, tok, d // 2), (tok, d // 4)
        scat = []
        for half in (half1, half2):
            scat += [pltpu.VMEM(half, f32)] * 2 + [pltpu.VMEM((2,) + half, f32)] * 2
        y_rows, gx_rows, grad_wg, grad_wu, grad_wd, _, _ = pl.pallas_call(
            mlp_kernel,
            out_shape=[sds((tok, d), bf16), sds((tok, d), bf16), sds((d_loc, ff), f32), sds((d_loc, ff), f32),
                       sds((ff, d_loc), f32), spread, spread],
            in_specs=[vmem] * 2 + [hbm] * 3,
            out_specs=[vmem] * 2 + [hbm] * 5,
            scratch_shapes=[pltpu.VMEM((d, ff), bf16)] * 2 + [pltpu.VMEM((ff, d), bf16)]
            + [pltpu.VMEM((RING, RING, tok, d), bf16)] * 2 + [whole] * 3
            + [pltpu.VMEM((up_rows, ff), f32)] * 2 + [pltpu.VMEM((ff, d_loc), f32)]
            + [pltpu.VMEM((RING, RING, tok, d), f32)] * 2 + scat * 4
            + [pltpu.SemaphoreType.DMA((n_sem,)), pltpu.SemaphoreType.DMA((n_sem,)), pltpu.SemaphoreType.DMA((32,))],
            compiler_params=pltpu.CompilerParams(collective_id=0, has_side_effects=True, vmem_limit_bytes=67043328),
            name="mlp",
        )(x_loc, gy_loc, wg_loc, wu_loc, wd_loc)
        return y_rows, gx_rows, grad_wg, grad_wu, grad_wd

    row_spec = P(("dp", "tp"), None)
    up_spec = P("dp", "tp")
    down_spec = P("tp", "dp")
    return jax.shard_map(local_step, mesh=mesh,
                         in_specs=(row_spec, up_spec, up_spec, down_spec, row_spec),
                         out_specs=(row_spec, row_spec, up_spec, up_spec, down_spec),
                         check_vma=False)
```

time: 565 us -> 208 us (0.37)
  waiting for transfers between devices: 441 us -> 0 us
  Pallas kernels: 0 us -> 197 us
  matrix products: 55.6 us -> 0 us
  blocking collectives: 19.3 us -> 0 us
  between operations: 13.9 us -> 0.64 us
  starting transfers between devices: 10.4 us -> 0 us
  other arithmetic: 8.36 us -> 0 us
    pallas_call x0 -> x1, Pallas kernels: none -> 197 us  [local_step(): pl.pallas_call(mlp_kernel, out_shape=[sds((tok, d), bf16), sds((tok, d),...]
    all_gather x5 -> x0, waiting for transfers between devices: 158 us -> none  [the longest x2 72.9 us: spread_cols(): gathered = lax.all_gather(cols_mine, 'tp', axis=1)]
    reduce_scatter x3 -> x0, waiting for transfers between devices: 150 us -> none  [the longest x1 54.5 us: local_step(): lax.psum_scatter(jnp.dot(x_cols, wu_loc, preferred_element_type=jnp.float...]
    unnamed x10 -> x0, waiting for transfers between devices: 130 us -> none
    dot_general x9 -> x0, matrix products: 55.6 us -> none  [the longest x1 7.85 us: local_step(): jnp.einsum('nf,df->nd', up_all, wu_loc, preferred_element_type=jnp.float32)]
    all_to_all x2 -> x0, blocking collectives: 19.3 us -> none  [spread_cols(): cols_mine = lax.all_to_all(rows_loc, 'dp', 1, 0, tiled=True)]
    all_to_all x2 -> x0, starting transfers between devices: 9.86 us -> none  [collect_rows(): lax.all_to_all(summed.astype(jnp.bfloat16), 'dp', 0, 2, tiled=True)]
    convert_element_type x3 -> x0, other arithmetic: 8.36 us -> none  [the longest x2 4.52 us: collect_rows(): summed.astype(jnp.bfloat16)]
  transfers between devices with their start and end apart: 11 -> 0, of which waited for: 10 -> 0; matrix products, arithmetic and copies ran while one was open for 11% -> 0% of each run, Pallas kernels for 0% -> 0%
where the time goes in v2:
time: 208 us
  Pallas kernels  197 us (95%)
  local copies, waits for them, and re-layouts  10.1 us (5%)
    pallas_call x1, Pallas kernels, local_step(): pl.pallas_call(mlp_kernel, out_shape=[sds((tok, d), bf16), sds((tok, d),...  197 us
    unnamed x9, local copies, waits for them, and re-layouts  10.1 us

profile of v2, /device:TPU:1, one launch (start us, length us, event | category | flops | bytes accessed | tf_op | source)
XLA Modules:
  0.0 207.6 jit_solution(9850033819182606833)
XLA Ops:
  0.6 196.9 %mlp.1 = (bf16[16,4096]{1,0:T(8,128)(2,1)}, bf16[16,4096]{1,0:T(8,128)(2,1)}, f32[512,1024]{1,0:T(8,128)}, f32[512,1024]{1,0:T(8,128)}, f32[1024,512]{1,0:T(8,12...) custom-call(bf16[16,4096]{1,0:T(8,128)(2,1)} %x_ref.1, bf16[16,4096]{1,0:T(8,128)(2,1)} %gy_ref.1, ...), custom_call_target="tpu_custom_call" | custom-call | tf_op jit(solution)/shard_map/mlp/pallas_call | solution.py:500
  197.5 1.6 copy.15
  199.1 1.6 copy.16
  200.6 0.0 copy-start.1
  200.6 3.3 %copy.17 = f32[512,1024]{1,0:T(8,128)} copy(f32[512,1024]{1,0:T(8,128)} %get-tuple-element.22) | data formatting | bytes 4194304
  204.0 0.0 copy-done.1
  204.0 0.0 copy-start
  204.0 1.3 copy.18
  205.3 1.0 copy-done
  206.3 1.3 copy.19
Async XLA Ops:
  200.6 3.3 %copy-start.1 = (f32[512,1024]{1,0:T(8,128)S(1)}, f32[512,1024]{1,0:T(8,128)}, u32[]{:S(2)}) copy-start(f32[512,1024]{1,0:T(8,128)} %get-tuple-element.23) | copy-start | bytes 6291460
  204.0 2.3 %copy-start = (f32[1024,512]{1,0:T(8,128)S(1)}, f32[1024,512]{1,0:T(8,128)}, u32[]{:S(2)}) copy-start(f32[1024,512]{1,0:T(8,128)} %get-tuple-element.24) | copy-start | bytes 6291460

commit v3 on v2

v3 whole, which is shorter than its diff:
```python
import itertools

import jax
import jax.numpy as jnp
from jax import lax
from jax.experimental import pallas as pl
from jax.experimental.pallas import tpu as pltpu
from jax.sharding import PartitionSpec as P

RING = 4
N_DP = 2 * RING
VMEM = pltpu.MemorySpace.VMEM


class Links:
    def __init__(self, send_sem, recv_sem, local_sem):
        self.send_sem, self.recv_sem, self.local_sem = send_sem, recv_sem, local_sem
        self.n_remote = self.n_local = 0
        self.sent, self.local = [], []
        dp, tp = lax.axis_index("dp"), lax.axis_index("tp")
        self.dp, self.tp = dp, tp
        self.x, self.core = dp // 2, dp % 2
        self.z, self.y = tp // RING, tp % RING
        odd = self.x % 2
        self.xa = self.x + 1 - 2 * odd
        self.xb = (self.x + 3 + 2 * odd) % RING

    def at(self, pos, off):
        return (pos + off) % RING

    def device(self, axis, off):
        if axis == "x":
            return {"dp": 2 * self.at(self.x, off) + self.core, "tp": self.tp}
        if axis == "a":
            return {"dp": 2 * self.xa + self.core, "tp": self.tp}
        if axis == "b":
            return {"dp": 2 * self.xb + self.core, "tp": self.tp}
        if axis == "block":
            return {"dp": off, "tp": self.tp}
        if axis == "core":
            return {"dp": 2 * self.x + (1 - self.core), "tp": self.tp}
        if axis == "dp":
            return {"dp": (self.dp + off) % N_DP, "tp": self.tp}
        if axis == "z":
            return {"dp": self.dp, "tp": RING * self.at(self.z, off) + self.y}
        return {"dp": self.dp, "tp": RING * self.z + self.at(self.y, off)}

    def barrier(self, peers):
        sem = pltpu.get_barrier_semaphore()
        for axis, off in peers:
            pl.semaphore_signal(sem, inc=1, device_id=self.device(axis, off),
                                device_id_type=pl.DeviceIdType.MESH)
        pl.semaphore_wait(sem, len(peers))

    def send(self, src, dst, axis, off=0):
        k = self.n_remote
        self.n_remote += 1
        copy = pltpu.make_async_remote_copy(
            src_ref=src, dst_ref=dst, send_sem=self.send_sem.at[k], recv_sem=self.recv_sem.at[k],
            device_id=self.device(axis, off), device_id_type=pl.DeviceIdType.MESH)
        copy.start()
        self.sent.append(copy)
        return copy

    def put(self, src, dst):
        k = self.n_local
        self.n_local += 1
        copy = pltpu.make_async_copy(src, dst, self.local_sem.at[k])
        copy.start()
        self.local.append(copy)
        return copy

    def sent_all(self):
        for copy in self.sent:
            copy.wait_send()
        self.sent = []

    def put_all(self):
        for copy in self.local:
            copy.wait()
        self.local = []


def gather_start(links, own, block, axis, pos):
    right = links.send(own, block(pos, None), axis, 1)
    left = links.send(own, block(pos, None), axis, -1)
    return right, left


def gather_forward(links, copies, block, axis, pos):
    copies[0].wait_recv()
    from_left = links.at(pos, -1)
    right = links.send(block(from_left, 0), block(from_left, 0), axis, 1)
    copies[1].wait_recv()
    from_right = links.at(pos, 1)
    left = links.send(block(from_right, 1), block(from_right, 1), axis, -1)
    return right, left


def gather_end(copies):
    for copy in copies:
        copy.wait_recv()


class DpGather:
    def __init__(self, links, own, slot):
        self.links, self.slot = links, slot
        x, c = links.x, links.core
        self.block = lambda p, h: slot(2 * p + c, h)
        self.ring = gather_start(links, own, self.block, "x", x)
        self.mate = [links.send(own, slot(links.dp, None), "core")]

    def forward(self):
        links = self.links
        self.ring = gather_forward(links, self.ring, self.block, "x", links.x)
        for off in (-1, 1):
            b = self.block(links.at(links.x, off), None)
            self.mate.append(links.send(b, b, "core"))

    def near(self):
        gather_end(self.mate)
        self.mate = []

    def far(self):
        links = self.links
        far = links.at(links.x, 2)
        for h in (0, 1):
            self.ring[h].wait_recv()
            b = self.block(far, h)
            self.mate.append(links.send(b, b, "core"))


class PairGather:
    def __init__(self, links, own, slots):
        self.links, self.slots = links, slots
        c = links.core
        self.pair = [links.send(own(h), slots[h](2 + c), "ab"[h]) for h in (0, 1)]
        self.mate = [links.send(own(h), slots[h](c), "core") for h in (0, 1)]
        for h in (0, 1):
            links.put(own(h), slots[h](c))

    def forward(self):
        links = self.links
        for h in (0, 1):
            self.pair[h].wait_recv()
            s = self.slots[h](2 + links.core)
            self.mate.append(links.send(s, s, "core"))

    def near(self):
        gather_end(self.mate)


class Scatter:
    def __init__(self, links, part, slots, z_first, bufs):
        self.links, z, y = links, links.z, links.y
        half = part.shape[-1] // 2
        self.slots = slots
        n = pl.ds(slots[0], len(slots))
        if z_first:
            self.axes, self.pos = ("z", "y"), (z, y)
            first = lambda p, h: part.at[n, p, pl.ds(2 * h, 2)]
            second = lambda p, h: part.at[n, z, p, :, pl.ds(h * half, half)]
        else:
            self.axes, self.pos = ("y", "z"), (y, z)
            first = lambda p, h: part.at[n, pl.ds(2 * h, 2), p]
            second = lambda p, h: part.at[n, p, y, :, pl.ds(h * half, half)]
        self.block = (first, second)
        self.bufs = (bufs[:4], bufs[4:])

    def start(self, phase):
        links, block, axis, pos = self.links, self.block[phase], self.axes[phase], self.pos[phase]
        near0, near1, l_ref, r_ref = self.bufs[phase]
        far = links.at(pos, 2)
        self.first = (links.send(block(far, 0), near0, axis, 1), links.send(block(far, 1), near1, axis, -1))
        self.last = [links.send(block(links.at(pos, 1), 1), l_ref.at[1], axis, 1),
                     links.send(block(links.at(pos, -1), 0), r_ref.at[0], axis, -1)]

    def forward(self, phase):
        links, block, axis, pos = self.links, self.block[phase], self.axes[phase], self.pos[phase]
        near0, near1, l_ref, r_ref = self.bufs[phase]
        for copy, off, h, near, dst in ((self.first[0], 1, 0, near0, l_ref), (self.first[1], -1, 1, near1, r_ref)):
            copy.wait_recv()
            b = block(links.at(pos, off), h)
            add_into(b, [near])
            self.last.append(links.send(b, dst.at[h], axis, off))

    def end(self, phase):
        block, pos = self.block[phase], self.pos[phase]
        _, _, l_ref, r_ref = self.bufs[phase]
        gather_end(self.last)
        for h in (0, 1):
            add_into(block(pos, h), [l_ref.at[h], r_ref.at[h]])


TILE = 256


def add_into(dst, terms):
    for lead in itertools.product(*(range(n) for n in dst.shape[:-2])):
        total = dst[lead]
        for t in terms:
            total = total + t[lead]
        dst[lead] = total


def loop(n, body):
    def step(i, carry):
        body(i)
        return carry
    lax.fori_loop(0, n, step, 0)


def part_of(i, size):
    return pl.ds(pl.multiple_of(i * size, size), size)


NN = (((1,), (0,)), ((), ()))
NT = (((1,), (1,)), ((), ()))
TN = (((0,), (0,)), ((), ()))


def dot(a, b, dims):
    return lax.dot_general(a, b, dims, preferred_element_type=jnp.float32)


OWN, OWN_A, OWN_B, TOK_B, TOK_A, SECTIONS = 0, 2, 4, 6, 10, 14


def mlp_kernel(x_ref, gy_ref, wg_ref, wu_ref, wd_ref,
               y_ref, gx_ref, gwg_ref, gwu_ref, gwd_ref, xc_ref, gc_ref,
               wga, wgb, wua, wub, wda, wdb, xr, gr, xm, gm, q_out, q_in, ha, daa, dba,
               acc_g, acc_u, acc_d, y_part, gx_part, y_stage, gx_stage, *rest):
    scat_bufs, (send_sem, recv_sem, local_sem) = rest[:-3], rest[-3:]
    links = Links(send_sem, recv_sem, local_sem)
    dp, z, y, x, core = links.dp, links.z, links.y, links.x, links.core
    tok, d = x_ref.shape
    d_loc, ff = wg_ref.shape
    ffh = ff // 2
    rows = RING * RING * tok
    bf16 = x_ref.dtype
    links.barrier([("dp", o) for o in range(1, N_DP)] + [("z", 1), ("z", -1), ("y", 1), ("y", -1)])

    def d_of(ref, j, n=1):
        return ref.at[:, part_of(j, n * d_loc)]

    def section(ref, s, n):
        return ref.at[z, y, :, pl.ds(s * d_loc, n * d_loc)]

    def spread(src, dst):
        return [links.send(d_of(src, (dp + o) % N_DP), dst.at[dp], "dp", o) for o in range(1, N_DP)]

    opp = links.at(x, 2)

    def lend(src, dst):
        return [links.send(d_of(src, links.xb, 2), section(dst, TOK_B, 2), "b"),
                links.send(d_of(src, opp, 2), section(dst, TOK_B + 2, 2), "b"),
                links.send(d_of(src, links.xa, 2), section(dst, TOK_A, 2), "a"),
                links.send(d_of(src, opp, 2), section(dst, TOK_A + 2, 2), "a")]

    lent = [lend(x_ref, xr), lend(gy_ref, gr)]
    spreads = [spread(x_ref, xm), spread(gy_ref, gm)]
    gate = PairGather(links, lambda h: wg_ref.at[:, pl.ds(h * ffh, ffh)],
                      [lambda k: wga.at[part_of(k, d_loc)], lambda k: wgb.at[part_of(k, d_loc)]])
    up = PairGather(links, lambda h: wu_ref.at[:, pl.ds(h * ffh, ffh)],
                    [lambda k: wua.at[part_of(k, d_loc)], lambda k: wub.at[part_of(k, d_loc)]])
    down = PairGather(links, lambda h: wd_ref.at[pl.ds(h * ffh, ffh)],
                      [lambda k: wda.at[:, part_of(k, d_loc)], lambda k: wdb.at[:, part_of(k, d_loc)]])
    for src, dst, mine in ((x_ref, xr, xm), (gy_ref, gr, gm)):
        for s, j in ((OWN, x), (OWN_A, links.xa), (OWN_B, links.xb)):
            dst[z, y, :, s * d_loc:(s + 2) * d_loc] = src[:, part_of(j, 2 * d_loc)]
        mine[dp] = src[:, part_of(dp, d_loc)]

    row_half = SECTIONS * d_loc // 2

    def half_of(h):
        return pl.ds(h * row_half, row_half)

    def dp_half(h):
        return pl.ds(h * (N_DP // 2), N_DP // 2)

    def xr_first(p, h):
        return xr.at[p, y] if h is None else xr.at[p, y, :, half_of(h)]

    def xr_second(p, h):
        return xr.at[:, p] if h is None else xr.at[pl.ds(2 * h, 2), p]

    def gr_first(p, h):
        return gr.at[z, p] if h is None else gr.at[z, p, :, half_of(h)]

    def gr_second(p, h):
        return gr.at[p] if h is None else gr.at[p, pl.ds(2 * h, 2)]

    def xc_first(p, h):
        return xc_ref.at[:, p, y] if h is None else xc_ref.at[dp_half(h), p, y]

    def xc_second(p, h):
        return xc_ref.at[:, :, p] if h is None else xc_ref.at[dp_half(h), :, p]

    def gc_first(p, h):
        return gc_ref.at[:, z, p] if h is None else gc_ref.at[dp_half(h), z, p]

    def gc_second(p, h):
        return gc_ref.at[:, p] if h is None else gc_ref.at[dp_half(h), p]

    row_sends = []

    def start(own, block, axis, pos):
        copies = gather_start(links, own, block, axis, pos)
        row_sends.extend(copies)
        return copies

    def forward(copies, block, axis, pos):
        copies = gather_forward(links, copies, block, axis, pos)
        row_sends.extend(copies)
        return copies

    gather_end(lent[0])
    rx = start(xr_first(z, None), xr_first, "z", z)
    gather_end(lent[1])
    rg = start(gr_first(y, None), gr_first, "y", y)
    for copies in spreads:
        gather_end(copies)
    links.put_all()
    own_cols = [links.put(xm, xc_first(z, None)), links.put(gm, gc_first(y, None))]
    rx = forward(rx, xr_first, "z", z)
    rg = forward(rg, gr_first, "y", y)
    gather_end(rx)
    rx = start(xr_second(y, None), xr_second, "y", y)
    gather_end(rg)
    rg = start(gr_second(z, None), gr_second, "z", z)
    gate.forward()
    rx = forward(rx, xr_second, "y", y)
    rg = forward(rg, gr_second, "z", z)
    links.put_all()
    cx = gather_start(links, xm, xc_first, "z", z)
    cg = gather_start(links, gm, gc_first, "y", y)
    up.forward()
    gather_end(rx)

    accs = (acc_g.at[pl.ds(0, rows)], acc_g.at[pl.ds(rows, rows)], acc_u.at[pl.ds(0, rows)])
    tile = min(TILE, ffh)
    n_tile = ffh // tile

    def take(ref, s, n):
        return ref[:, :, :, s * d_loc:(s + n) * d_loc].reshape(rows, n * d_loc)

    def product(src, s, n, w, first, t, down_side):
        if down_side:
            return dot(take(src, s, n), w[t, first * d_loc:(first + n) * d_loc], NT)
        return dot(take(src, s, n), w[first * d_loc:(first + n) * d_loc, t], NN)

    def lend_sums(k, src, wa, wb, down_side):
        def body(i):
            t = part_of(i, tile)
            q_out[k, 0, :, t] = product(src, TOK_B, 4, wa, 0, t, down_side)
            q_out[k, 1, :, t] = product(src, TOK_A, 4, wb, 0, t, down_side)
        loop(n_tile, body)
        return [links.send(q_out.at[k, 0], q_in.at[k, 0], "b"), links.send(q_out.at[k, 1], q_in.at[k, 1], "a")]

    def own_sums(k, src, wa, wb, down_side):
        def body(i):
            t = part_of(i, tile)
            accs[k][:, t] = product(src, OWN, 4, wa, 0, t, down_side)
            accs[k][:, part_of(i + n_tile, tile)] = (product(src, OWN, 2, wb, 0, t, down_side)
                                                     + product(src, OWN_B, 2, wb, 2, t, down_side))
        loop(n_tile, body)

    gate.near()
    qa = lend_sums(0, xr, wga, wgb, False)
    up.near()
    qb = lend_sums(1, xr, wua, wub, False)
    gather_end(rg)
    down.forward()
    down.near()
    qg = lend_sums(2, gr, wda, wdb, True)
    cx = gather_forward(links, cx, xc_first, "z", z)
    cg = gather_forward(links, cg, gc_first, "y", y)
    own_sums(0, xr, wga, wgb, False)
    own_sums(1, xr, wua, wub, False)
    gather_end(cx)
    cx = gather_start(links, xc_second(y, None), xc_second, "y", y)
    gather_end(cg)
    cg = gather_start(links, gc_second(z, None), gc_second, "z", z)
    own_sums(2, gr, wda, wdb, True)

    step_rows = 16

    def gate_loop(body):
        def step(i):
            r = part_of(i, step_rows)
            own = part_of(dp * (rows // step_rows) + i, step_rows)
            for h in (0, 1):
                cols = pl.ds(h * ffh, ffh)
                body(own, cols, lambda k: accs[k][r, cols] + q_in[k, h, r])
        loop(rows // step_rows, step)

    def hidden_body(own, cols, value):
        a = value(0)
        ha[own, cols] = (a * jax.nn.sigmoid(a) * value(1)).astype(bf16)

    gather_end(qa)
    gather_end(qb)
    gate_loop(hidden_body)
    mine = part_of(dp, rows)

    def row_slot(ref):
        def slot(j, h):
            if h is None:
                return ref.at[part_of(j, rows)]
            return ref.at[part_of(2 * j + h, rows // 2)]
        return slot

    hid = DpGather(links, ha.at[mine], row_slot(ha))
    cx = gather_forward(links, cx, xc_second, "y", y)
    cg = gather_forward(links, cg, gc_second, "z", z)

    def grad_body(own, cols, value):
        a, g = value(0), value(2)
        s = jax.nn.sigmoid(a)
        daa[own, cols] = (g * value(1) * (s * (1.0 + a * (1.0 - s)))).astype(bf16)
        dba[own, cols] = (g * (a * s)).astype(bf16)

    gather_end(qg)
    gate_loop(grad_body)
    dgate = DpGather(links, daa.at[mine], row_slot(daa))
    dup = DpGather(links, dba.at[mine], row_slot(dba))

    gather_end(cx)
    gather_end(cg)
    for copy in row_sends:
        copy.wait_send()
    links.sent = [c for c in links.sent if not any(c is r for r in row_sends)]
    for j in range(N_DP):
        links.put(xc_ref.at[j], xr.at[:, :, :, pl.ds(j * d_loc, d_loc)])
        links.put(gc_ref.at[j], gr.at[:, :, :, pl.ds(j * d_loc, d_loc)])

    def clear(*refs):
        for ref in refs:
            n, step = ref.shape[0], min(16, ref.shape[0])

            def body(i):
                ref[part_of(i, step)] = jnp.zeros((step, ref.shape[1]), jnp.float32)
            loop(n // step, body)

    clear(acc_g, acc_u, acc_d)

    def block_of(s):
        far = s // 6
        q = s % 3
        chip = (1 - far) * (q + q // 2) + far * 2
        other = (1 - far) * ((s // 3) % 2) + far * (s % 2)
        return 2 * ((x + chip) % RING) + (core + other) % 2

    d_tile = min(TILE, d_loc)
    n_d = d_loc // d_tile
    ff_tile = min(TILE, ff)
    n_ff = ff // ff_tile
    low, high = pl.ds(0, ffh), pl.ds(ffh, ffh)
    torus = (RING, RING, tok)

    def y_blocks(lo, n):
        def body(i):
            s = lo + i // n_d
            r, t = part_of(block_of(s), rows), part_of(i % n_d, d_tile)
            w = part_of(core * n_d + i % n_d, d_tile)
            y_part[s, :, :, :, t] = (dot(ha[r, low], wda[:, w], NN) + dot(ha[r, high], wdb[:, w], NN)).reshape(
                torus + (d_tile,))
        loop(n * n_d, body)

    def gx_blocks(lo, n):
        def body(i):
            s = lo + i // n_d
            r, t = part_of(block_of(s), rows), part_of(i % n_d, d_tile)
            w = part_of(core * n_d + i % n_d, d_tile)
            gx_part[s, :, :, :, t] = (dot(daa[r, low], wga[w], NT) + dot(daa[r, high], wgb[w], NT)
                                      + dot(dba[r, low], wua[w], NT) + dot(dba[r, high], wub[w], NT)).reshape(
                torus + (d_tile,))
        loop(n * n_d, body)

    def cols_of(ref, j):
        return ref[:, :, :, part_of(j, d_loc)].reshape(rows, d_loc)

    def add_wd(lo, n):
        def body(i):
            j, t = block_of(lo + i // n_ff), part_of(i % n_ff, ff_tile)
            acc_d[t] += dot(ha[part_of(j, rows), t], cols_of(gr, j), TN)
        loop(n * n_ff, body)

    def add_wup(acc, src, lo, n):
        def body(i):
            j, t = block_of(lo + i // n_ff), part_of(i % n_ff, ff_tile)
            acc[pl.ds(0, d_loc), t] += dot(cols_of(xr, j), src[part_of(j, rows), t], TN)
        loop(n * n_ff, body)

    n_buf = 8

    def units(part, k):
        bufs = [scat_bufs[(4 * k + u) * n_buf:(4 * k + u + 1) * n_buf] for u in range(4)]
        near = [Scatter(links, part, (0, 1, 2), True, bufs[0]), Scatter(links, part, (3, 4, 5), False, bufs[1])]
        return near, [Scatter(links, part, (6,), True, bufs[2]), Scatter(links, part, (7,), False, bufs[3])]

    y_near, y_far = units(y_part, 0)
    g_near, g_far = units(gx_part, 1)
    returns = []

    def finish(group, part, resid, stage, out):
        for unit in group:
            unit.end(1)
            for s in unit.slots:
                j = block_of(s)
                piece = (resid[j].astype(jnp.float32) + part[s, z, y]).astype(bf16)
                if s == 0:
                    out[:, part_of(dp, d_loc)] = piece
                else:
                    stage[s] = piece
        for unit in group:
            for s in unit.slots:
                if s:
                    returns.append(links.send(stage.at[s], out.at[:, part_of(dp, d_loc)], "block", block_of(s)))

    def each(group, *steps):
        for name, phase in steps:
            for unit in group:
                getattr(unit, name)(phase)

    hid.forward()
    hid.near()
    y_blocks(0, 6)
    each(y_near, ("start", 0))
    links.put_all()
    add_wd(0, 6)
    each(y_near, ("forward", 0))
    dgate.forward()
    each(y_near, ("end", 0), ("start", 1))
    dup.forward()
    dgate.near()
    dup.near()
    gx_blocks(0, 6)
    each(g_near, ("start", 0))
    each(y_near, ("forward", 1))
    hid.far()
    hid.near()
    y_blocks(6, 2)
    each(y_far, ("start", 0))
    add_wup(acc_g, daa, 0, 6)
    each(g_near, ("forward", 0))
    finish(y_near, y_part, xm, y_stage, y_ref)
    dgate.far()
    each(y_far, ("forward", 0))
    add_wup(acc_u, dba, 0, 6)
    dup.far()
    dgate.near()
    dup.near()
    gx_blocks(6, 2)
    each(g_far, ("start", 0))
    each(y_far, ("end", 0), ("start", 1))
    add_wd(6, 2)
    links.put(acc_d, gwd_ref)
    each(g_near, ("end", 0), ("start", 1))
    each(g_far, ("forward", 0))
    each(y_far, ("forward", 1))
    add_wup(acc_g, daa, 6, 2)
    links.put(acc_g.at[pl.ds(0, d_loc)], gwg_ref)
    each(g_far, ("end", 0), ("start", 1))
    each(g_near, ("forward", 1))
    each(g_far, ("forward", 1))
    finish(y_far, y_part, xm, y_stage, y_ref)
    finish(g_near, gx_part, gm, gx_stage, gx_ref)
    finish(g_far, gx_part, gm, gx_stage, gx_ref)
    add_wup(acc_u, dba, 6, 2)
    links.put(acc_u.at[pl.ds(0, d_loc)], gwu_ref)
    gather_end(returns)
    links.sent_all()
    links.put_all()


PIECES = 4


def copy_kernel(*refs):
    n = (len(refs) - 2) // 3
    ins, outs, bufs, (in_sem, out_sem) = refs[:n], refs[n:2 * n], refs[2 * n:3 * n], refs[3 * n:]
    loads, stores = [], []
    for k in range(n):
        pieces = PIECES if ins[k].shape[0] >= 128 else 1
        size = ins[k].shape[0] // pieces
        for p in range(pieces):
            part, sem = pl.ds(p * size, size), k * PIECES + p
            loads.append(pltpu.make_async_copy(ins[k].at[part], bufs[k].at[part], in_sem.at[sem]))
            stores.append(pltpu.make_async_copy(bufs[k].at[part], outs[k].at[part], out_sem.at[sem]))
    for load in loads:
        load.start()
    for load, store in zip(loads, stores):
        load.wait()
        store.start()
    for store in stores:
        store.wait()


def solution(mesh):
    vmem = pl.BlockSpec(memory_space=VMEM)
    hbm = pl.BlockSpec(memory_space=pl.ANY)

    def local_step(x_loc, wg_loc, wu_loc, wd_loc, gy_loc):
        tok, d = x_loc.shape
        d_loc, ff = wg_loc.shape
        ffh = ff // 2
        bf16, f32 = x_loc.dtype, jnp.float32
        sds = jax.ShapeDtypeStruct
        n_sem = 224
        rows = RING * RING * tok
        spread = sds((N_DP, RING, RING, tok, d_loc), bf16)
        up_rows = max(d_loc, 2 * rows)
        whole = pltpu.VMEM((N_DP * rows, ff), bf16)
        mine = pltpu.VMEM((N_DP, tok, d_loc), bf16)
        scat = []
        for n in (3, 3, 1, 1):
            for half in ((n, 2, tok, d_loc), (n, tok, d_loc // 2)):
                scat += [pltpu.VMEM(half, f32)] * 2 + [pltpu.VMEM((2,) + half, f32)] * 2
        results = [sds((tok, d), bf16), sds((tok, d), bf16), sds((d_loc, ff), f32), sds((d_loc, ff), f32),
                   sds((ff, d_loc), f32)]
        outs = pl.pallas_call(
            mlp_kernel,
            out_shape=results + [spread, spread],
            in_specs=[vmem] * 2 + [hbm] * 3,
            out_specs=[vmem] * 2 + [hbm] * 5,
            scratch_shapes=[pltpu.VMEM((4 * d_loc, ffh), bf16)] * 4 + [pltpu.VMEM((ffh, 4 * d_loc), bf16)] * 2
            + [pltpu.VMEM((RING, RING, tok, SECTIONS * d_loc), bf16)] * 2 + [mine] * 2
            + [pltpu.VMEM((3, 2, rows, ffh), f32)] * 2 + [whole] * 3
            + [pltpu.VMEM((up_rows, ff), f32)] * 2 + [pltpu.VMEM((ff, d_loc), f32)]
            + [pltpu.VMEM((N_DP, RING, RING, tok, d_loc), f32)] * 2 + [mine] * 2 + scat * 2
            + [pltpu.SemaphoreType.DMA((n_sem,)), pltpu.SemaphoreType.DMA((n_sem,)), pltpu.SemaphoreType.DMA((32,))],
            compiler_params=pltpu.CompilerParams(collective_id=0, has_side_effects=True, vmem_limit_bytes=67043328),
            name="mlp",
        )(x_loc, gy_loc, wg_loc, wu_loc, wd_loc)[:5]
        return pl.pallas_call(
            copy_kernel,
            out_shape=results,
            in_specs=[hbm] * 5,
            out_specs=[hbm] * 5,
            scratch_shapes=[pltpu.VMEM(r.shape, r.dtype) for r in results]
            + [pltpu.SemaphoreType.DMA((5 * PIECES,))] * 2,
            name="results",
        )(*outs)

    row_spec = P(("dp", "tp"), None)
    up_spec = P("dp", "tp")
    down_spec = P("tp", "dp")
    return jax.shard_map(local_step, mesh=mesh,
                         in_specs=(row_spec, up_spec, up_spec, down_spec, row_spec),
                         out_specs=(row_spec, row_spec, up_spec, up_spec, down_spec),
                         check_vma=False)
```

time: 208 us -> 191 us (0.918)
  local copies, waits for them, and re-layouts: 10.1 us -> 0 us
  Pallas kernels: 197 us -> 190 us
    unnamed x9 -> x0, local copies, waits for them, and re-layouts: 10.1 us -> none
    pallas_call x1 -> x2, Pallas kernels: 197 us -> 190 us  [the longest x1 185 us: local_step(): pl.pallas_call(mlp_kernel, out_shape=results + [spread, spread], in_specs...]
where the time goes in v3:
time: 191 us
  Pallas kernels  190 us (99%)
    pallas_call x1, Pallas kernels, local_step(): pl.pallas_call(mlp_kernel, out_shape=results + [spread, spread], in_specs...  185 us
    pallas_call x1, Pallas kernels, local_step(): pl.pallas_call(copy_kernel, out_shape=results, in_specs=[hbm] * 5, out_sp...  5.67 us

profile of v3, /device:TPU:1, one launch (start us, length us, event | category | flops | bytes accessed | tf_op | source)
XLA Modules:
  0.0 191.0 jit_solution(714046555484411126)
XLA Ops:
  0.6 184.6 %mlp.1 = (bf16[16,4096]{1,0:T(8,128)(2,1)}, bf16[16,4096]{1,0:T(8,128)(2,1)}, f32[512,1024]{1,0:T(8,128)}, f32[512,1024]{1,0:T(8,128)}, f32[1024,512]{1,0:T(8,12...) custom-call(bf16[16,4096]{1,0:T(8,128)(2,1)} %x_ref.1, bf16[16,4096]{1,0:T(8,128)(2,1)} %gy_ref.1, ...), custom_call_target="tpu_custom_call" | custom-call | tf_op jit(solution)/shard_map/mlp/pallas_call | solution.py:622
  185.3 5.7 %results.1 = (bf16[16,4096]{1,0:T(8,128)(2,1)}, bf16[16,4096]{1,0:T(8,128)(2,1)}, f32[512,1024]{1,0:T(8,128)}, f32[512,1024]{1,0:T(8,128)}, f32[1024,512]{1,0:T(8,128)}) custom-call(bf16[16,4096]{1,0:T(8,128)(2,1)} %get-tuple-element.10.refs_0_, bf16[16,4096]{1,0:T(8,128)(2,1)} %get-tuple-element.11.refs_1_, f32[512,1024]{1,0:T(8,128)} %get-tuple-element.12.refs_2_, ...), custom_call_target="tpu_custom_call" | custom-call | tf_op jit(solution)/shard_map/results/pallas_call | solution.py:636

commit v4 on v3

--- a/solution.py
+++ b/solution.py
@@ -150,6 +150,35 @@
         gather_end(self.mate)
 
 
+class Rows:
+    def __init__(self, links, ref, lo, width, z_first):
+        self.links, z, y = links, links.z, links.y
+        half = width // 2
+        cols = pl.ds(lo, width)
+        if z_first:
+            self.axes, self.pos = ("z", "y"), (z, y)
+            first = lambda p, h: ref.at[p, y, :, cols if h is None else pl.ds(lo + h * half, half)]
+            second = lambda p, h: ref.at[slice(None) if h is None else pl.ds(2 * h, 2), p, :, cols]
+        else:
+            self.axes, self.pos = ("y", "z"), (y, z)
+            first = lambda p, h: ref.at[z, p, :, cols if h is None else pl.ds(lo + h * half, half)]
+            second = lambda p, h: ref.at[p, slice(None) if h is None else pl.ds(2 * h, 2), :, cols]
+        self.block = (first, second)
+        self.sent = []
+
+    def start(self, phase):
+        block, pos = self.block[phase], self.pos[phase]
+        self.copies = gather_start(self.links, block(pos, None), block, self.axes[phase], pos)
+        self.sent.extend(self.copies)
+
+    def forward(self, phase):
+        self.copies = gather_forward(self.links, self.copies, self.block[phase], self.axes[phase], self.pos[phase])
+        self.sent.extend(self.copies)
+
+    def end(self, phase):
+        gather_end(self.copies)
+
+
 class Scatter:
     def __init__(self, links, part, slots, z_first, bufs):
         self.links, z, y = links, links.z, links.y
@@ -258,11 +287,11 @@
                 links.send(d_of(src, opp, 2), section(dst, TOK_A + 2, 2), "a")]
 
     lent = [lend(x_ref, xr), lend(gy_ref, gr)]
-    spreads = [spread(x_ref, xm), spread(gy_ref, gm)]
     gate = PairGather(links, lambda h: wg_ref.at[:, pl.ds(h * ffh, ffh)],
                       [lambda k: wga.at[part_of(k, d_loc)], lambda k: wgb.at[part_of(k, d_loc)]])
     up = PairGather(links, lambda h: wu_ref.at[:, pl.ds(h * ffh, ffh)],
                     [lambda k: wua.at[part_of(k, d_loc)], lambda k: wub.at[part_of(k, d_loc)]])
+    spreads = [spread(x_ref, xm), spread(gy_ref, gm)]
     down = PairGather(links, lambda h: wd_ref.at[pl.ds(h * ffh, ffh)],
                       [lambda k: wda.at[:, part_of(k, d_loc)], lambda k: wdb.at[:, part_of(k, d_loc)]])
     for src, dst, mine in ((x_ref, xr, xm), (gy_ref, gr, gm)):
@@ -270,26 +299,18 @@
             dst[z, y, :, s * d_loc:(s + 2) * d_loc] = src[:, part_of(j, 2 * d_loc)]
         mine[dp] = src[:, part_of(dp, d_loc)]
 
+    def each(group, *steps):
+        for name, phase in steps:
+            for unit in group:
+                getattr(unit, name)(phase)
+
     row_half = SECTIONS * d_loc // 2
-
-    def half_of(h):
-        return pl.ds(h * row_half, row_half)
+    x_rows = [Rows(links, xr, 0, row_half, True), Rows(links, xr, row_half, row_half, False)]
+    g_rows = [Rows(links, gr, 0, row_half, True), Rows(links, gr, row_half, row_half, False)]
 
     def dp_half(h):
         return pl.ds(h * (N_DP // 2), N_DP // 2)
 
-    def xr_first(p, h):
-        return xr.at[p, y] if h is None else xr.at[p, y, :, half_of(h)]
-
-    def xr_second(p, h):
-        return xr.at[:, p] if h is None else xr.at[pl.ds(2 * h, 2), p]
-
-    def gr_first(p, h):
-        return gr.at[z, p] if h is None else gr.at[z, p, :, half_of(h)]
-
-    def gr_second(p, h):
-        return gr.at[p] if h is None else gr.at[p, pl.ds(2 * h, 2)]
-
     def xc_first(p, h):
         return xc_ref.at[:, p, y] if h is None else xc_ref.at[dp_half(h), p, y]
 
@@ -302,40 +323,16 @@
     def gc_second(p, h):
         return gc_ref.at[:, p] if h is None else gc_ref.at[dp_half(h), p]
 
-    row_sends = []
-
-    def start(own, block, axis, pos):
-        copies = gather_start(links, own, block, axis, pos)
-        row_sends.extend(copies)
-        return copies
-
-    def forward(copies, block, axis, pos):
-        copies = gather_forward(links, copies, block, axis, pos)
-        row_sends.extend(copies)
-        return copies
-
     gather_end(lent[0])
-    rx = start(xr_first(z, None), xr_first, "z", z)
+    each(x_rows, ("start", 0))
     gather_end(lent[1])
-    rg = start(gr_first(y, None), gr_first, "y", y)
-    for copies in spreads:
-        gather_end(copies)
+    each(x_rows, ("forward", 0), ("end", 0), ("start", 1))
+    each(g_rows, ("start", 0))
+    each(x_rows, ("forward", 1))
     links.put_all()
-    own_cols = [links.put(xm, xc_first(z, None)), links.put(gm, gc_first(y, None))]
-    rx = forward(rx, xr_first, "z", z)
-    rg = forward(rg, gr_first, "y", y)
-    gather_end(rx)
-    rx = start(xr_second(y, None), xr_second, "y", y)
-    gather_end(rg)
-    rg = start(gr_second(z, None), gr_second, "z", z)
     gate.forward()
-    rx = forward(rx, xr_second, "y", y)
-    rg = forward(rg, gr_second, "z", z)
-    links.put_all()
-    cx = gather_start(links, xm, xc_first, "z", z)
-    cg = gather_start(links, gm, gc_first, "y", y)
-    up.forward()
-    gather_end(rx)
+    each(g_rows, ("forward", 0), ("end", 0), ("start", 1))
+    each(x_rows, ("end", 1))
 
     accs = (acc_g.at[pl.ds(0, rows)], acc_g.at[pl.ds(rows, rows)], acc_u.at[pl.ds(0, rows)])
     tile = min(TILE, ffh)
@@ -367,21 +364,26 @@
 
     gate.near()
     qa = lend_sums(0, xr, wga, wgb, False)
+    up.forward()
     up.near()
     qb = lend_sums(1, xr, wua, wub, False)
-    gather_end(rg)
+    for copies in spreads:
+        gather_end(copies)
+    links.put(xm, xc_first(z, None))
+    links.put(gm, gc_first(y, None))
+    each(g_rows, ("forward", 1))
+    cx = gather_start(links, xm, xc_first, "z", z)
+    cg = gather_start(links, gm, gc_first, "y", y)
+    own_sums(0, xr, wga, wgb, False)
+    own_sums(1, xr, wua, wub, False)
     down.forward()
+    each(g_rows, ("end", 1))
     down.near()
     qg = lend_sums(2, gr, wda, wdb, True)
     cx = gather_forward(links, cx, xc_first, "z", z)
     cg = gather_forward(links, cg, gc_first, "y", y)
-    own_sums(0, xr, wga, wgb, False)
-    own_sums(1, xr, wua, wub, False)
-    gather_end(cx)
-    cx = gather_start(links, xc_second(y, None), xc_second, "y", y)
-    gather_end(cg)
-    cg = gather_start(links, gc_second(z, None), gc_second, "z", z)
     own_sums(2, gr, wda, wdb, True)
+    links.put_all()
 
     step_rows = 16
 
@@ -411,8 +413,10 @@
         return slot
 
     hid = DpGather(links, ha.at[mine], row_slot(ha))
-    cx = gather_forward(links, cx, xc_second, "y", y)
-    cg = gather_forward(links, cg, gc_second, "z", z)
+    gather_end(cx)
+    cx = gather_start(links, xc_second(y, None), xc_second, "y", y)
+    gather_end(cg)
+    cg = gather_start(links, gc_second(z, None), gc_second, "z", z)
 
     def grad_body(own, cols, value):
         a, g = value(0), value(2)
@@ -425,14 +429,8 @@
     dgate = DpGather(links, daa.at[mine], row_slot(daa))
     dup = DpGather(links, dba.at[mine], row_slot(dba))
 
-    gather_end(cx)
-    gather_end(cg)
-    for copy in row_sends:
-        copy.wait_send()
-    links.sent = [c for c in links.sent if not any(c is r for r in row_sends)]
-    for j in range(N_DP):
-        links.put(xc_ref.at[j], xr.at[:, :, :, pl.ds(j * d_loc, d_loc)])
-        links.put(gc_ref.at[j], gr.at[:, :, :, pl.ds(j * d_loc, d_loc)])
+    cx = gather_forward(links, cx, xc_second, "y", y)
+    cg = gather_forward(links, cg, gc_second, "z", z)
 
     def clear(*refs):
         for ref in refs:
@@ -518,57 +516,63 @@
                 if s:
                     returns.append(links.send(stage.at[s], out.at[:, part_of(dp, d_loc)], "block", block_of(s)))
 
-    def each(group, *steps):
-        for name, phase in steps:
-            for unit in group:
-                getattr(unit, name)(phase)
-
     hid.forward()
+
+    gather_end(cx)
+    gather_end(cg)
+    row_sends = [copy for rows_of in x_rows + g_rows for copy in rows_of.sent]
+    for copy in row_sends:
+        copy.wait_send()
+    links.sent = [c for c in links.sent if not any(c is r for r in row_sends)]
+    for j in range(N_DP):
+        links.put(xc_ref.at[j], xr.at[:, :, :, pl.ds(j * d_loc, d_loc)])
+        links.put(gc_ref.at[j], gr.at[:, :, :, pl.ds(j * d_loc, d_loc)])
+
     hid.near()
     y_blocks(0, 6)
     each(y_near, ("start", 0))
+    dgate.forward()
+    each(y_near, ("forward", 0))
     links.put_all()
     add_wd(0, 6)
-    each(y_near, ("forward", 0))
-    dgate.forward()
+    dgate.near()
+    add_wup(acc_g, daa, 0, 6)
+    dup.forward()
     each(y_near, ("end", 0), ("start", 1))
-    dup.forward()
-    dgate.near()
     dup.near()
     gx_blocks(0, 6)
     each(g_near, ("start", 0))
+    hid.far()
     each(y_near, ("forward", 1))
-    hid.far()
     hid.near()
     y_blocks(6, 2)
     each(y_far, ("start", 0))
-    add_wup(acc_g, daa, 0, 6)
     each(g_near, ("forward", 0))
+    add_wup(acc_u, dba, 0, 6)
+    dgate.far()
     finish(y_near, y_part, xm, y_stage, y_ref)
-    dgate.far()
     each(y_far, ("forward", 0))
-    add_wup(acc_u, dba, 0, 6)
     dup.far()
     dgate.near()
     dup.near()
     gx_blocks(6, 2)
     each(g_far, ("start", 0))
-    each(y_far, ("end", 0), ("start", 1))
     add_wd(6, 2)
     links.put(acc_d, gwd_ref)
     each(g_near, ("end", 0), ("start", 1))
-    each(g_far, ("forward", 0))
-    each(y_far, ("forward", 1))
     add_wup(acc_g, daa, 6, 2)
     links.put(acc_g.at[pl.ds(0, d_loc)], gwg_ref)
+    each(g_far, ("forward", 0))
+    each(y_far, ("end", 0), ("start", 1))
+    each(g_near, ("forward", 1))
+    add_wup(acc_u, dba, 6, 2)
+    links.put(acc_u.at[pl.ds(0, d_loc)], gwu_ref)
     each(g_far, ("end", 0), ("start", 1))
-    each(g_near, ("forward", 1))
+    each(y_far, ("forward", 1))
     each(g_far, ("forward", 1))
     finish(y_far, y_part, xm, y_stage, y_ref)
     finish(g_near, gx_part, gm, gx_stage, gx_ref)
     finish(g_far, gx_part, gm, gx_stage, gx_ref)
-    add_wup(acc_u, dba, 6, 2)
-    links.put(acc_u.at[pl.ds(0, d_loc)], gwu_ref)
     gather_end(returns)
     links.sent_all()
     links.put_all()
@@ -607,7 +611,7 @@
         ffh = ff // 2
         bf16, f32 = x_loc.dtype, jnp.float32
         sds = jax.ShapeDtypeStruct
-        n_sem = 224
+        n_sem = 240
         rows = RING * RING * tok
         spread = sds((N_DP, RING, RING, tok, d_loc), bf16)
         up_rows = max(d_loc, 2 * rows)

time: 191 us -> 180 us (0.942)
  Pallas kernels: 190 us -> 179 us
    pallas_call x1, Pallas kernels: 185 us -> 174 us  [local_step(): pl.pallas_call(mlp_kernel, out_shape=results + [spread, spread], in_specs...]
where the time goes in v4:
time: 180 us
  Pallas kernels  179 us (99%)
    pallas_call x1, Pallas kernels, local_step(): pl.pallas_call(mlp_kernel, out_shape=results + [spread, spread], in_specs...  174 us
    pallas_call x1, Pallas kernels, local_step(): pl.pallas_call(copy_kernel, out_shape=results, in_specs=[hbm] * 5, out_sp...  5.67 us

profile of v4, /device:TPU:1, one launch (start us, length us, event | category | flops | bytes accessed | tf_op | source)
XLA Modules:
  0.0 179.8 jit_solution(9852903541376935746)
XLA Ops:
  0.6 173.5 %mlp.1 = (bf16[16,4096]{1,0:T(8,128)(2,1)}, bf16[16,4096]{1,0:T(8,128)(2,1)}, f32[512,1024]{1,0:T(8,128)}, f32[512,1024]{1,0:T(8,128)}, f32[1024,512]{1,0:T(8,12...) custom-call(bf16[16,4096]{1,0:T(8,128)(2,1)} %x_ref.1, bf16[16,4096]{1,0:T(8,128)(2,1)} %gy_ref.1, ...), custom_call_target="tpu_custom_call" | custom-call | tf_op jit(solution)/shard_map/mlp/pallas_call | solution.py:626
  174.1 5.7 %results.1 = (bf16[16,4096]{1,0:T(8,128)(2,1)}, bf16[16,4096]{1,0:T(8,128)(2,1)}, f32[512,1024]{1,0:T(8,128)}, f32[512,1024]{1,0:T(8,128)}, f32[1024,512]{1,0:T(8,128)}) custom-call(bf16[16,4096]{1,0:T(8,128)(2,1)} %get-tuple-element.10.refs_0_, bf16[16,4096]{1,0:T(8,128)(2,1)} %get-tuple-element.11.refs_1_, f32[512,1024]{1,0:T(8,128)} %get-tuple-element.12.refs_2_, ...), custom_call_target="tpu_custom_call" | custom-call | tf_op jit(solution)/shard_map/results/pallas_call | solution.py:640

commit v5 on v4

--- a/solution.py
+++ b/solution.py
@@ -116,6 +116,10 @@
         for off in (-1, 1):
             b = self.block(links.at(links.x, off), None)
             self.mate.append(links.send(b, b, "core"))
+
+    def own(self):
+        gather_end(self.mate[:1])
+        self.mate = self.mate[1:]
 
     def near(self):
         gather_end(self.mate)
@@ -443,11 +447,8 @@
     clear(acc_g, acc_u, acc_d)
 
     def block_of(s):
-        far = s // 6
-        q = s % 3
-        chip = (1 - far) * (q + q // 2) + far * 2
-        other = (1 - far) * ((s // 3) % 2) + far * (s % 2)
-        return 2 * ((x + chip) % RING) + (core + other) % 2
+        p = s // 2
+        return 2 * ((x + p + p // 2 - 2 * (p // 3)) % RING) + (core + s) % 2
 
     d_tile = min(TILE, d_loc)
     n_d = d_loc // d_tile
@@ -491,14 +492,15 @@
         loop(n * n_ff, body)
 
     n_buf = 8
+    groups = ((0,), (1,)), ((2, 3), (4, 5)), ((6,), (7,))
 
     def units(part, k):
-        bufs = [scat_bufs[(4 * k + u) * n_buf:(4 * k + u + 1) * n_buf] for u in range(4)]
-        near = [Scatter(links, part, (0, 1, 2), True, bufs[0]), Scatter(links, part, (3, 4, 5), False, bufs[1])]
-        return near, [Scatter(links, part, (6,), True, bufs[2]), Scatter(links, part, (7,), False, bufs[3])]
-
-    y_near, y_far = units(y_part, 0)
-    g_near, g_far = units(gx_part, 1)
+        bufs = [scat_bufs[(6 * k + u) * n_buf:(6 * k + u + 1) * n_buf] for u in range(6)]
+        return [[Scatter(links, part, pair[i], i == 0, bufs[2 * n + i]) for i in (0, 1)]
+                for n, pair in enumerate(groups)]
+
+    y_own, y_near, y_far = units(y_part, 0)
+    g_own, g_near, g_far = units(gx_part, 1)
     returns = []
 
     def finish(group, part, resid, stage, out):
@@ -516,8 +518,15 @@
                 if s:
                     returns.append(links.send(stage.at[s], out.at[:, part_of(dp, d_loc)], "block", block_of(s)))
 
+    for gathered in (hid, dgate, dup):
+        gathered.own()
+    y_blocks(0, 2)
+    each(y_own, ("start", 0))
+    each(y_own, ("forward", 0))
     hid.forward()
-
+    hid.near()
+    y_blocks(2, 4)
+    each(y_near, ("start", 0))
     gather_end(cx)
     gather_end(cg)
     row_sends = [copy for rows_of in x_rows + g_rows for copy in rows_of.sent]
@@ -527,52 +536,57 @@
     for j in range(N_DP):
         links.put(xc_ref.at[j], xr.at[:, :, :, pl.ds(j * d_loc, d_loc)])
         links.put(gc_ref.at[j], gr.at[:, :, :, pl.ds(j * d_loc, d_loc)])
-
-    hid.near()
-    y_blocks(0, 6)
-    each(y_near, ("start", 0))
+    gx_blocks(0, 2)
+    each(g_own, ("start", 0))
     dgate.forward()
-    each(y_near, ("forward", 0))
     links.put_all()
     add_wd(0, 6)
+    each(y_near, ("forward", 0))
     dgate.near()
     add_wup(acc_g, daa, 0, 6)
+    each(y_near, ("end", 0), ("start", 1))
+    each(y_own, ("end", 0), ("start", 1))
     dup.forward()
-    each(y_near, ("end", 0), ("start", 1))
+    each(g_own, ("forward", 0))
+    each(y_near, ("forward", 1))
     dup.near()
-    gx_blocks(0, 6)
+    gx_blocks(2, 4)
     each(g_near, ("start", 0))
     hid.far()
-    each(y_near, ("forward", 1))
+    add_wup(acc_u, dba, 0, 6)
     hid.near()
+    each(g_own, ("end", 0), ("start", 1))
     y_blocks(6, 2)
     each(y_far, ("start", 0))
     each(g_near, ("forward", 0))
-    add_wup(acc_u, dba, 0, 6)
+    finish(y_near, y_part, xm, y_stage, y_ref)
+    each(y_own, ("forward", 1))
+    add_wd(6, 2)
+    links.put(acc_d, gwd_ref)
+    each(g_own, ("forward", 1))
     dgate.far()
-    finish(y_near, y_part, xm, y_stage, y_ref)
     each(y_far, ("forward", 0))
+    dgate.near()
     dup.far()
-    dgate.near()
     dup.near()
     gx_blocks(6, 2)
     each(g_far, ("start", 0))
-    add_wd(6, 2)
-    links.put(acc_d, gwd_ref)
-    each(g_near, ("end", 0), ("start", 1))
     add_wup(acc_g, daa, 6, 2)
     links.put(acc_g.at[pl.ds(0, d_loc)], gwg_ref)
+    each(y_far, ("end", 0), ("start", 1))
+    finish(y_own, y_part, xm, y_stage, y_ref)
     each(g_far, ("forward", 0))
-    each(y_far, ("end", 0), ("start", 1))
+    each(y_far, ("forward", 1))
+    each(g_near, ("end", 0), ("start", 1))
+    each(g_far, ("end", 0), ("start", 1))
+    finish(y_far, y_part, xm, y_stage, y_ref)
     each(g_near, ("forward", 1))
+    each(g_far, ("forward", 1))
+    finish(g_own, gx_part, gm, gx_stage, gx_ref)
+    finish(g_near, gx_part, gm, gx_stage, gx_ref)
+    finish(g_far, gx_part, gm, gx_stage, gx_ref)
     add_wup(acc_u, dba, 6, 2)
     links.put(acc_u.at[pl.ds(0, d_loc)], gwu_ref)
-    each(g_far, ("end", 0), ("start", 1))
-    each(y_far, ("forward", 1))
-    each(g_far, ("forward", 1))
-    finish(y_far, y_part, xm, y_stage, y_ref)
-    finish(g_near, gx_part, gm, gx_stage, gx_ref)
-    finish(g_far, gx_part, gm, gx_stage, gx_ref)
     gather_end(returns)
     links.sent_all()
     links.put_all()
@@ -611,14 +625,14 @@
         ffh = ff // 2
         bf16, f32 = x_loc.dtype, jnp.float32
         sds = jax.ShapeDtypeStruct
-        n_sem = 240
+        n_sem = 288
         rows = RING * RING * tok
         spread = sds((N_DP, RING, RING, tok, d_loc), bf16)
         up_rows = max(d_loc, 2 * rows)
         whole = pltpu.VMEM((N_DP * rows, ff), bf16)
         mine = pltpu.VMEM((N_DP, tok, d_loc), bf16)
         scat = []
-        for n in (3, 3, 1, 1):
+        for n in (1, 1, 2, 2, 1, 1):
             for half in ((n, 2, tok, d_loc), (n, tok, d_loc // 2)):
                 scat += [pltpu.VMEM(half, f32)] * 2 + [pltpu.VMEM((2,) + half, f32)] * 2
         results = [sds((tok, d), bf16), sds((tok, d), bf16), sds((d_loc, ff), f32), sds((d_loc, ff), f32),

time: 180 us -> 177 us (0.983)
  Pallas kernels: 179 us -> 176 us
    pallas_call x1, Pallas kernels: 174 us -> 170 us  [local_step(): pl.pallas_call(mlp_kernel, out_shape=results + [spread, spread], in_specs...]
where the time goes in v5:
time: 177 us
  Pallas kernels  176 us (99%)
    pallas_call x1, Pallas kernels, local_step(): pl.pallas_call(mlp_kernel, out_shape=results + [spread, spread], in_specs...  170 us
    pallas_call x1, Pallas kernels, local_step(): pl.pallas_call(copy_kernel, out_shape=results, in_specs=[hbm] * 5, out_sp...  5.67 us

profile of v5, /device:TPU:1, one launch (start us, length us, event | category | flops | bytes accessed | tf_op | source)
XLA Modules:
  0.0 176.7 jit_solution(272137791325604194)
XLA Ops:
  0.6 170.4 %mlp.1 = (bf16[16,4096]{1,0:T(8,128)(2,1)}, bf16[16,4096]{1,0:T(8,128)(2,1)}, f32[512,1024]{1,0:T(8,128)}, f32[512,1024]{1,0:T(8,128)}, f32[1024,512]{1,0:T(8,12...) custom-call(bf16[16,4096]{1,0:T(8,128)(2,1)} %x_ref.1, bf16[16,4096]{1,0:T(8,128)(2,1)} %gy_ref.1, ...), custom_call_target="tpu_custom_call" | custom-call | tf_op jit(solution)/shard_map/mlp/pallas_call | solution.py:640
  171.0 5.7 %results.1 = (bf16[16,4096]{1,0:T(8,128)(2,1)}, bf16[16,4096]{1,0:T(8,128)(2,1)}, f32[512,1024]{1,0:T(8,128)}, f32[512,1024]{1,0:T(8,128)}, f32[1024,512]{1,0:T(8,128)}) custom-call(bf16[16,4096]{1,0:T(8,128)(2,1)} %get-tuple-element.10.refs_0_, bf16[16,4096]{1,0:T(8,128)(2,1)} %get-tuple-element.11.refs_1_, f32[512,1024]{1,0:T(8,128)} %get-tuple-element.12.refs_2_, ...), custom_call_target="tpu_custom_call" | custom-call | tf_op jit(solution)/shard_map/results/pallas_call | solution.py:654

commit v6 on v5

--- a/solution.py
+++ b/solution.py
@@ -260,9 +260,9 @@
 
 
 def mlp_kernel(x_ref, gy_ref, wg_ref, wu_ref, wd_ref,
-               y_ref, gx_ref, gwg_ref, gwu_ref, gwd_ref, xc_ref, gc_ref,
+               y_ref, gx_ref, acc_g, acc_u, acc_d, xc_ref, gc_ref,
                wga, wgb, wua, wub, wda, wdb, xr, gr, xm, gm, q_out, q_in, ha, daa, dba,
-               acc_g, acc_u, acc_d, y_part, gx_part, y_stage, gx_stage, *rest):
+               y_part, gx_part, y_stage, gx_stage, *rest):
     scat_bufs, (send_sem, recv_sem, local_sem) = rest[:-3], rest[-3:]
     links = Links(send_sem, recv_sem, local_sem)
     dp, z, y, x, core = links.dp, links.z, links.y, links.x, links.core
@@ -562,7 +562,6 @@
     finish(y_near, y_part, xm, y_stage, y_ref)
     each(y_own, ("forward", 1))
     add_wd(6, 2)
-    links.put(acc_d, gwd_ref)
     each(g_own, ("forward", 1))
     dgate.far()
     each(y_far, ("forward", 0))
@@ -572,7 +571,6 @@
     gx_blocks(6, 2)
     each(g_far, ("start", 0))
     add_wup(acc_g, daa, 6, 2)
-    links.put(acc_g.at[pl.ds(0, d_loc)], gwg_ref)
     each(y_far, ("end", 0), ("start", 1))
     finish(y_own, y_part, xm, y_stage, y_ref)
     each(g_far, ("forward", 0))
@@ -586,33 +584,22 @@
     finish(g_near, gx_part, gm, gx_stage, gx_ref)
     finish(g_far, gx_part, gm, gx_stage, gx_ref)
     add_wup(acc_u, dba, 6, 2)
-    links.put(acc_u.at[pl.ds(0, d_loc)], gwu_ref)
     gather_end(returns)
     links.sent_all()
     links.put_all()
 
 
-PIECES = 4
+VMEM_LIMIT = 56 * 1024 * 1024
 
 
 def copy_kernel(*refs):
-    n = (len(refs) - 2) // 3
-    ins, outs, bufs, (in_sem, out_sem) = refs[:n], refs[n:2 * n], refs[2 * n:3 * n], refs[3 * n:]
-    loads, stores = [], []
-    for k in range(n):
-        pieces = PIECES if ins[k].shape[0] >= 128 else 1
-        size = ins[k].shape[0] // pieces
-        for p in range(pieces):
-            part, sem = pl.ds(p * size, size), k * PIECES + p
-            loads.append(pltpu.make_async_copy(ins[k].at[part], bufs[k].at[part], in_sem.at[sem]))
-            stores.append(pltpu.make_async_copy(bufs[k].at[part], outs[k].at[part], out_sem.at[sem]))
-    for load in loads:
-        load.start()
-    for load, store in zip(loads, stores):
-        load.wait()
-        store.start()
-    for store in stores:
-        store.wait()
+    n = (len(refs) - 1) // 2
+    ins, outs, sem = refs[:n], refs[n:2 * n], refs[-1]
+    copies = [pltpu.make_async_copy(ins[k], outs[k], sem.at[k]) for k in range(n)]
+    for copy in copies:
+        copy.start()
+    for copy in copies:
+        copy.wait()
 
 
 def solution(mesh):
@@ -628,7 +615,7 @@
         n_sem = 288
         rows = RING * RING * tok
         spread = sds((N_DP, RING, RING, tok, d_loc), bf16)
-        up_rows = max(d_loc, 2 * rows)
+        assert d_loc == 2 * rows
         whole = pltpu.VMEM((N_DP * rows, ff), bf16)
         mine = pltpu.VMEM((N_DP, tok, d_loc), bf16)
         scat = []
@@ -639,25 +626,24 @@
                    sds((ff, d_loc), f32)]
         outs = pl.pallas_call(
             mlp_kernel,
-            out_shape=results + [spread, spread],
+            out_shape=[VMEM(r.shape, r.dtype) for r in results] + [spread, spread],
             in_specs=[vmem] * 2 + [hbm] * 3,
-            out_specs=[vmem] * 2 + [hbm] * 5,
+            out_specs=[vmem] * 5 + [hbm] * 2,
             scratch_shapes=[pltpu.VMEM((4 * d_loc, ffh), bf16)] * 4 + [pltpu.VMEM((ffh, 4 * d_loc), bf16)] * 2
             + [pltpu.VMEM((RING, RING, tok, SECTIONS * d_loc), bf16)] * 2 + [mine] * 2
             + [pltpu.VMEM((3, 2, rows, ffh), f32)] * 2 + [whole] * 3
-            + [pltpu.VMEM((up_rows, ff), f32)] * 2 + [pltpu.VMEM((ff, d_loc), f32)]
             + [pltpu.VMEM((N_DP, RING, RING, tok, d_loc), f32)] * 2 + [mine] * 2 + scat * 2
             + [pltpu.SemaphoreType.DMA((n_sem,)), pltpu.SemaphoreType.DMA((n_sem,)), pltpu.SemaphoreType.DMA((32,))],
-            compiler_params=pltpu.CompilerParams(collective_id=0, has_side_effects=True, vmem_limit_bytes=67043328),
+            compiler_params=pltpu.CompilerParams(collective_id=0, has_side_effects=True, vmem_limit_bytes=VMEM_LIMIT),
             name="mlp",
         )(x_loc, gy_loc, wg_loc, wu_loc, wd_loc)[:5]
         return pl.pallas_call(
             copy_kernel,
             out_shape=results,
-            in_specs=[hbm] * 5,
+            in_specs=[vmem] * 5,
             out_specs=[hbm] * 5,
-            scratch_shapes=[pltpu.VMEM(r.shape, r.dtype) for r in results]
-            + [pltpu.SemaphoreType.DMA((5 * PIECES,))] * 2,
+            scratch_shapes=[pltpu.SemaphoreType.DMA((5,))],
+            compiler_params=pltpu.CompilerParams(vmem_limit_bytes=16 * 1024 * 1024),
             name="results",
         )(*outs)
 

time: 177 us -> 173 us (0.977)
  Pallas kernels: 176 us -> 172 us
    pallas_call x2, Pallas kernels: 176 us -> 172 us  [the longest x1 170 us: local_step(): pl.pallas_call(mlp_kernel, out_shape=[VMEM(r.shape, r.dtype) for r in res...]
where the time goes in v6:
time: 173 us
  Pallas kernels  172 us (99%)
    pallas_call x1, Pallas kernels, local_step(): pl.pallas_call(mlp_kernel, out_shape=[VMEM(r.shape, r.dtype) for r in res...  170 us

profile of v6, /device:TPU:1, one launch (start us, length us, event | category | flops | bytes accessed | tf_op | source)
XLA Modules:
  0.0 173.1 jit_solution(2721371790134316884)
XLA Ops:
  0.6 169.7 %mlp.1 = (bf16[16,4096]{1,0:T(8,128)(2,1)S(1)}, bf16[16,4096]{1,0:T(8,128)(2,1)S(1)}, f32[512,1024]{1,0:T(8,128)S(1)}, f32[512,1024]{1,0:T(8,128)S(1)}, f32[1024...) custom-call(bf16[16,4096]{1,0:T(8,128)(2,1)} %x_ref.1, ...), custom_call_target="tpu_custom_call" | custom-call | tf_op jit(solution)/shard_map/mlp/pallas_call | solution.py:627
  170.3 2.8 %results.1 = (bf16[16,4096]{1,0:T(8,128)(2,1)}, bf16[16,4096]{1,0:T(8,128)(2,1)}, f32[512,1024]{1,0:T(8,128)}, f32[512,1024]{1,0:T(8,128)}, f32[1024,512]{1,0:T(8,128)}) custom-call(bf16[16,4096]{1,0:T(8,128)(2,1)S(1)} %get-tuple-element.10.refs_0_, bf16[16,4096]{1,0:T(8,128)(2,1)S(1)} %get-tuple-element.11.refs_1_, ...), custom_call_target="tpu_custom_call" | custom-call | tf_op jit(solution)/shard_map/results/pallas_call | solution.py:640
